TPU v7x, 32 devices: a 4x4x1 block of a 4x4x8 slice. The times are simulated.
32 devices in a mesh: dp: 1 (over z), pool: 4 (over y), ep: 8 (over x, core).
Axes of the slice: x: 4, y: 4, z: 1, core: 2. Of those that a mesh axis runs over, the one named last changes fastest.
The devices are a block of a 4x4x8 slice.
Arguments:
- hidden_in: bfloat16 [512, 1024], P(('dp', 'ep'))
- k_cache: bfloat16 [2, 512, 1024, 2, 128], P(None, ('dp', 'ep'), 'pool')
- v_cache: bfloat16 [2, 512, 1024, 2, 128], P(None, ('dp', 'ep'), 'pool')
- cache_len: int32 [512], P(('dp', 'ep'))
- w_q: bfloat16 [2, 1024, 1024], replicated
- w_k: bfloat16 [2, 1024, 256], replicated
- w_v: bfloat16 [2, 1024, 256], replicated
- w_o: bfloat16 [2, 1024, 1024], replicated
- w_router: float32 [2, 1024, 8], replicated
- expert_ids: int32 [2, 512, 2], P(None, ('dp', 'ep'))
- w_one: bfloat16 [2, 8, 1024, 3584], P(None, 'ep', None, 'pool')
- w_three: bfloat16 [2, 8, 1024, 3584], P(None, 'ep', None, 'pool')
- w_two: bfloat16 [2, 8, 3584, 1024], P(None, 'ep', 'pool')
Outputs:
- output: bfloat16 [512, 1024], P(('dp', 'ep'))
All inputs are finite; a program needn't handle non-finite values.
Results may differ from a plain program's by a relative error of at most 0.02.
Values are sent between devices in bfloat16 or wider.
A program may use at most 768 MiB of HBM per device.

v0:
```python
import jax
import jax.numpy as jnp
from jax import lax
from jax.sharding import PartitionSpec as P

NORM_EPS = 1e-6


def rms_norm(in_vals):
    in_vals = in_vals.astype(jnp.float32)
    return in_vals * lax.rsqrt(jnp.mean(in_vals * in_vals, axis=-1, keepdims=True) + NORM_EPS)


def attention_block(hidden, k_rows, v_rows, cache_len, w_q, w_k, w_v, w_o):
    tokens = hidden.shape[0]
    seq_local, kv_heads, head_dim = k_rows.shape[1], k_rows.shape[2], k_rows.shape[3]
    n_heads = w_q.shape[1] // head_dim
    q_group = n_heads // kv_heads
    att_scale = head_dim ** -0.5
    normed = rms_norm(hidden).astype(jnp.bfloat16)
    query = jnp.dot(normed, w_q, preferred_element_type=jnp.float32).astype(jnp.bfloat16).reshape(tokens, kv_heads, q_group, head_dim)
    key_new = jnp.dot(normed, w_k, preferred_element_type=jnp.float32).astype(jnp.bfloat16).reshape(tokens, kv_heads, head_dim)
    val_new = jnp.dot(normed, w_v, preferred_element_type=jnp.float32).astype(jnp.bfloat16).reshape(tokens, kv_heads, head_dim)
    score_vals = jnp.einsum('tgqd,tsgd->tgqs', query, k_rows, preferred_element_type=jnp.float32) * att_scale
    positions = lax.axis_index('pool') * seq_local + jnp.arange(seq_local)
    pos_mask = positions[None, :] < cache_len[:, None]
    score_vals = jnp.where(pos_mask[:, None, None, :], score_vals, -1e30)
    new_score = jnp.einsum('tgqd,tgd->tgq', query, key_new, preferred_element_type=jnp.float32) * att_scale
    top_score = jnp.maximum(lax.pmax(jnp.max(score_vals, axis=-1), 'pool'), new_score)
    prob_vals = jnp.exp(score_vals - top_score[..., None])
    new_prob = jnp.exp(new_score - top_score)
    denom_sum = lax.psum(jnp.sum(prob_vals, axis=-1), 'pool') + new_prob
    numer_sum = lax.psum(jnp.einsum('tgqs,tsgd->tgqd', prob_vals.astype(jnp.bfloat16), v_rows, preferred_element_type=jnp.float32), 'pool')
    numer_sum = numer_sum + new_prob[..., None] * val_new.astype(jnp.float32)[:, :, None, :]
    attn_out = (numer_sum / denom_sum[..., None]).astype(jnp.bfloat16).reshape(tokens, n_heads * head_dim)
    return (hidden.astype(jnp.float32) + jnp.dot(attn_out, w_o, preferred_element_type=jnp.float32)).astype(jnp.bfloat16)


def router_gates(resid_rows, w_router, ids_layer):
    normed = rms_norm(resid_rows).astype(jnp.bfloat16)
    logits = jnp.dot(normed.astype(jnp.float32), w_router, preferred_element_type=jnp.float32)
    gate_vals = jax.nn.softmax(jnp.take_along_axis(logits, ids_layer, axis=1), axis=-1)
    return normed, gate_vals


def expert_math(tok_rows, group_sizes, w_one, w_three, w_two):
    h_one = lax.ragged_dot(tok_rows, w_one, group_sizes, preferred_element_type=jnp.float32)
    h_three = lax.ragged_dot(tok_rows, w_three, group_sizes, preferred_element_type=jnp.float32)
    act_rows = (jax.nn.silu(h_one) * h_three).astype(jnp.bfloat16)
    part_out = lax.ragged_dot(act_rows, w_two, group_sizes, preferred_element_type=jnp.float32)
    return lax.psum(part_out, 'pool').astype(jnp.bfloat16)


def local_experts(recv_rows, recv_ids, w_one, w_three, w_two):
    n_local = w_one.shape[0]
    sort_order = jnp.argsort(recv_ids, stable=True)
    group_sizes = jnp.bincount(recv_ids, length=n_local).astype(jnp.int32)
    sorted_rows = jnp.take(recv_rows, sort_order, axis=0)
    expert_out = expert_math(sorted_rows, group_sizes, w_one, w_three, w_two)
    return jnp.take(expert_out, jnp.argsort(sort_order), axis=0)


def solution(mesh):
    n_dev = mesh.shape['ep']
    tok_spec = P(('dp', 'ep'), None)
    cache_spec = P(None, ('dp', 'ep'), 'pool', None, None)
    up_spec = P(None, 'ep', None, 'pool')
    down_spec = P(None, 'ep', 'pool', None)
    in_specs = (tok_spec, cache_spec, cache_spec, P(('dp', 'ep')), P(), P(), P(), P(), P(), P(None, ('dp', 'ep'), None), up_spec, up_spec, down_spec)

    def body(hidden_in, k_cache, v_cache, cache_len, w_q, w_k, w_v, w_o, w_router, expert_ids, w_one, w_three, w_two):
        hidden = hidden_in
        n_local = w_one.shape[1]
        for layer_idx in range(w_q.shape[0]):
            ids_layer = expert_ids[layer_idx]
            tokens, top_k = ids_layer.shape
            resid_rows = attention_block(hidden, k_cache[layer_idx], v_cache[layer_idx], cache_len, w_q[layer_idx], w_k[layer_idx], w_v[layer_idx], w_o[layer_idx])
            normed, gate_vals = router_gates(resid_rows, w_router[layer_idx], ids_layer)
            flat_ids = ids_layer.reshape(-1)
            send_order = jnp.argsort(flat_ids // n_local, stable=True)
            pair_pos = jnp.argsort(send_order)
            send_rows = jnp.take(normed, send_order // top_k, axis=0)
            send_ids = jnp.take(flat_ids % n_local, send_order)
            recv_rows = lax.all_to_all(send_rows, 'ep', 0, 0, tiled=True)
            recv_ids = lax.all_to_all(send_ids, 'ep', 0, 0, tiled=True)
            expert_rows = local_experts(recv_rows, recv_ids, w_one[layer_idx], w_three[layer_idx], w_two[layer_idx])
            back_rows = lax.all_to_all(expert_rows, 'ep', 0, 0, tiled=True)
            pair_rows = jnp.take(back_rows, pair_pos, axis=0).reshape(tokens, top_k, -1)
            mixed_sum = jnp.sum(gate_vals[..., None] * pair_rows.astype(jnp.float32), axis=1)
            hidden = (resid_rows.astype(jnp.float32) + mixed_sum).astype(jnp.bfloat16)
        return hidden

    return jax.shard_map(body, mesh=mesh, in_specs=in_specs, out_specs=tok_spec, check_vma=False)
```

profile of v0, /device:TPU:97, one launch (start us, length us, event | category | flops | bytes accessed | tf_op | source)
XLA Modules:
  0.0 361.7 jit_solution(4309967764646232676)
XLA Ops:
  7.6 2.2 fusion.36
  9.9 14.1 %fusion.92 = (bf16[1,64,256,2,128]{4,3,2,1,0:T(2,128)(2,1)}, bf16[1,64,256,2,128]{4,3,2,1,0:T(2,128)(2,1)}) fusion(bf16[2,64,256,2,128]{4,3,2,1,0:T(2,128)(2,1)} %param.22), kind=kLoop, calls=%fused_computation.181 | loop fusion | bytes 33554432 | tf_op jit(solution)/shard_map/slice | solution.py:77
  24.2 5.9 %fusion.95 = (f32[64,2,4]{2,1,0:T(2,128)S(1)}, f32[64,2,4,256]{3,2,1,0:T(4,128)S(1)}) fusion(bf16[64,2,4,128]{3,2,1,0:T(4,128)(2,1)S(1)} %reshape.170, bf16[1,64,256,2,128]{4,3,2,1,0:T(2,128)(2,1)} %get-tuple-element.64, pred[64,256]{1,0:T(8,128)(4,1)S(1)} %broadcast_compare_fusion), kind=kOutput, calls=%fused_computation.184 | convolution fusion | flops 33947136 | bytes 9062400 | tf_op jit(solution)/shard_map/tgqd,tsgd->tgqs/dot_general | solution.py:24
  30.0 16.5 %pmax.14 = f32[64,2,4]{2,1,0:T(2,128)S(1)} all-reduce(f32[64,2,4]{2,1,0:T(2,128)S(1)} %get-tuple-element.77), channel_id=1, replica_groups=mesh['dp'=1,'pool'=4,'ep'=8] {'pool'}, use_global_device_ids=true, to_apply=%region_2.3 | all-reduce | flops 512 | bytes 4096 | tf_op jit(solution)/shard_map/pmax | solution.py:29
  47.2 13.9 %fusion.93 = (bf16[1,64,256,2,128]{4,3,2,1,0:T(2,128)(2,1)S(1)}, bf16[1,64,256,2,128]{4,3,2,1,0:T(2,128)(2,1)}) fusion(bf16[2,64,256,2,128]{4,3,2,1,0:T(2,128)(2,1)} %param.23), kind=kLoop, calls=%fused_computation.182 | loop fusion | bytes 33554432 | tf_op jit(solution)/shard_map/slice | solution.py:77
  61.2 2.0 fusion.2
  63.5 2.5 sort.118
  68.0 8.9 %all-to-all-start.1 = ((s32[8,16,1]{1,2,0:T(1,128)}), s32[8,16,1]{1,2,0:T(1,128)S(1)}, u32[]{:S(2)}, u32[]{:S(2)}) async-start(s32[8,16,1]{1,2,0:T(1,128)} %bitcast.11), calls=%async_computation.1 | async-start | bytes 8192 | tf_op jit(solution)/shard_map/all_to_all | solution.py:85
  77.4 2.5 sort.121
  80.2 2.5 sort.122
  82.8 2.5 sort.125
  85.3 11.9 %psum.43 = f32[64,2,4]{2,1,0:T(2,128)S(1)} all-reduce(f32[64,2,4]{2,1,0:T(2,128)S(1)} %fusion.54), channel_id=1, replica_groups=mesh['dp'=1,'pool'=4,'ep'=8] {'pool'}, use_global_device_ids=true, to_apply=%region_5.6 | all-reduce | flops 512 | bytes 4096 | tf_op jit(solution)/shard_map/psum | solution.py:32
  97.6 4.4 %slice_bitcast_fusion.2 = (bf16[1,1024,896]{2,1,0:T(8,128)(2,1)}, bf16[1,1024,896]{2,1,0:T(8,128)(2,1)}) fusion(bf16[2,1,1024,896]{3,2,1,0:T(8,128)(2,1)} %param.31), kind=kLoop, calls=%fused_computation.36 | loop fusion | bytes 7340032 | tf_op jit(solution)/shard_map/squeeze | solution.py:86
  102.0 2.2 slice_bitcast_fusion.1
  105.4 2.2 slice_bitcast_fusion
  110.1 7.9 %all-to-all-start.4 = ((s32[8,16,1]{1,2,0:T(1,128)}), s32[8,16,1]{1,2,0:T(1,128)S(1)}, u32[]{:S(2)}, u32[]{:S(2)}) async-start(s32[8,16,1]{1,2,0:T(1,128)} %bitcast.31), calls=%async_computation.4 | async-start | bytes 8192 | tf_op jit(solution)/shard_map/all_to_all | solution.py:85
  119.2 2.6 sort.119
  121.8 2.6 sort.120
  125.2 2.5 sort.123
  127.8 2.5 sort.124
  130.4 2.6 scatter_fusion
  134.3 2.5 scatter_fusion.1
  139.4 2.2 multiply_reduce_fusion.3
  143.4 4.8 %all-to-all-start = ((bf16[8,16,1024]{2,1,0:T(8,128)(2,1)}), bf16[8,16,1024]{2,1,0:T(8,128)(2,1)S(1)}, u32[]{:S(2)}, u32[]{:S(2)}) async-start(bf16[8,16,1024]{2,1,0:T(8,128)(2,1)} %bitcast.13), calls=%async_computation | async-start | bytes 524288 | tf_op jit(solution)/shard_map/all_to_all | solution.py:84
  149.6 4.9 %all-to-all-done = bf16[8,16,1024]{2,1,0:T(8,128)(2,1)S(1)} async-done(((bf16[8,16,1024]{2,1,0:T(8,128)(2,1)}), bf16[8,16,1024]{2,1,0:T(8,128)(2,1)S(1)}, u32[]{:S(2)}, u32[]{:S(2)}) %all-to-all-start) | async-done | bytes 262176 | tf_op jit(solution)/shard_map/all_to_all | solution.py:84
  156.1 5.9 %ragged-dot-none.5 = f32[128,896]{1,0:T(8,128)} custom-call(s32[1]{0:T(128)} %get-tuple-element.37, s32[2]{0:T(128)} %get-tuple-element.38, s32[1]{0:T(128)} %get-tuple-element.39, s32[1]{0:T(128)} %get-tuple-element.40, s32[1]{0:T(128)} %get-tuple-element.37, bf16[128,1024]{1,0:T(8,128)(2,1)} %broadcast_select_fusion.4, bf16[1,1024,896]{2,1,0:T(8,128)(2,1)} %get-tuple-element.70), custom_call_target="tpu_custom_call" | custom-call | flops 234881024 | bytes 2555908 | tf_op jit(solution)/shard_map/ragged_dot_general/ragged-dot-none
  162.0 5.9 %ragged-dot-none.4 = f32[128,896]{1,0:T(8,128)} custom-call(s32[1]{0:T(128)} %get-tuple-element.37, s32[2]{0:T(128)} %get-tuple-element.38, s32[1]{0:T(128)} %get-tuple-element.39, s32[1]{0:T(128)} %get-tuple-element.40, s32[1]{0:T(128)} %get-tuple-element.37, bf16[128,1024]{1,0:T(8,128)(2,1)} %broadcast_select_fusion.4, bf16[1,1024,896]{2,1,0:T(8,128)(2,1)} %get-tuple-element.72), custom_call_target="tpu_custom_call" | custom-call | flops 234881024 | bytes 2555908 | tf_op jit(solution)/shard_map/ragged_dot_general/ragged-dot-none
  168.0 2.0 multiply_convert_fusion.1
  170.0 6.0 %ragged-dot-none.3 = f32[128,1024]{1,0:T(8,128)} custom-call(s32[1]{0:T(128)} %get-tuple-element.37, s32[2]{0:T(128)} %get-tuple-element.38, s32[1]{0:T(128)} %get-tuple-element.39, s32[1]{0:T(128)} %get-tuple-element.40, s32[1]{0:T(128)} %get-tuple-element.37, bf16[128,896]{1,0:T(8,128)(2,1)} %multiply_convert_fusion.1, bf16[1,896,1024]{2,1,0:T(8,128)(2,1)} %get-tuple-element.68), custom_call_target="tpu_custom_call" | custom-call | flops 234881024 | bytes 2588676 | tf_op jit(solution)/shard_map/ragged_dot_general/ragged-dot-none
  175.9 18.2 %all-reduce.8 = bf16[128,1024]{1,0:T(8,128)(2,1)S(1)} all-reduce(f32[128,1024]{1,0:T(8,128)} %ragged-dot-none.3), channel_id=1, replica_groups=mesh['dp'=1,'pool'=4,'ep'=8] {'pool'}, use_global_device_ids=true, to_apply=%region_12.17 | all-reduce | flops 131072 | bytes 786432 | tf_op jit(solution)/shard_map/psum | solution.py:51
  195.8 8.9 %all-to-all-start.2 = ((bf16[8,16,1024]{2,1,0:T(8,128)(2,1)}), bf16[8,16,1024]{2,1,0:T(8,128)(2,1)S(1)}, u32[]{:S(2)}, u32[]{:S(2)}) async-start(bf16[8,16,1024]{2,1,0:T(8,128)(2,1)} %bitcast.18), calls=%async_computation.2 | async-start | bytes 524288 | tf_op jit(solution)/shard_map/all_to_all | solution.py:87
  204.8 6.3 %all-to-all-done.2 = bf16[8,16,1024]{2,1,0:T(8,128)(2,1)S(1)} async-done(((bf16[8,16,1024]{2,1,0:T(8,128)(2,1)}), bf16[8,16,1024]{2,1,0:T(8,128)(2,1)S(1)}, u32[]{:S(2)}, u32[]{:S(2)}) %all-to-all-start.2) | async-done | bytes 262176 | tf_op jit(solution)/shard_map/all_to_all | solution.py:87
  214.8 2.1 fusion.39
  217.3 5.8 %fusion.96 = (f32[64,2,4]{2,1,0:T(2,128)S(1)}, f32[64,2,4,256]{3,2,1,0:T(4,128)S(1)}) fusion(bf16[64,2,4,128]{3,2,1,0:T(4,128)(2,1)S(1)} %reshape.173, bf16[1,64,256,2,128]{4,3,2,1,0:T(2,128)(2,1)} %get-tuple-element.63, pred[64,256]{1,0:T(8,128)(4,1)S(1)} %broadcast_compare_fusion), kind=kOutput, calls=%fused_computation.185 | convolution fusion | flops 33947136 | bytes 9062400 | tf_op jit(solution)/shard_map/tgqd,tsgd->tgqs/dot_general | solution.py:24
  223.1 11.6 %pmax.15 = f32[64,2,4]{2,1,0:T(2,128)S(1)} all-reduce(f32[64,2,4]{2,1,0:T(2,128)S(1)} %get-tuple-element.81), channel_id=1, replica_groups=mesh['dp'=1,'pool'=4,'ep'=8] {'pool'}, use_global_device_ids=true, to_apply=%region_18.23 | all-reduce | flops 512 | bytes 4096 | tf_op jit(solution)/shard_map/pmax | solution.py:29
  234.8 5.4 %fusion = f32[64,2,4,128]{3,2,1,0:T(4,128)} fusion(bf16[1,64,256,2,128]{4,3,2,1,0:T(2,128)(2,1)} %get-tuple-element.66, f32[64,2,4,256]{3,2,1,0:T(4,128)S(1)} %get-tuple-element.82, f32[64,2,4]{2,1,0:T(2,128)S(1)} %multiply_maximum_fusion), kind=kOutput, calls=%fused_computation.15 | convolution fusion | flops 33816576 | bytes 9177088 | tf_op jit(solution)/shard_map/tgqs,tsgd->tgqd/dot_general | solution.py:33
  240.7 12.8 %psum.46 = f32[64,2,4]{2,1,0:T(2,128)S(1)} all-reduce(f32[64,2,4]{2,1,0:T(2,128)S(1)} %fusion.56), channel_id=1, replica_groups=mesh['dp'=1,'pool'=4,'ep'=8] {'pool'}, use_global_device_ids=true, to_apply=%region_21.26 | all-reduce | flops 512 | bytes 4096 | tf_op jit(solution)/shard_map/psum | solution.py:32
  253.6 23.5 %all-reduce.7.cloned.1.call-done = f32[64,2,4,128]{3,2,1,0:T(4,128)} async-done(((f32[64,2,4,128]{3,2,1,0:T(4,128)}), f32[64,2,4,128]{3,2,1,0:T(4,128)}) %all-reduce.7.cloned.1.call-update) | async-done | bytes 262160 | tf_op jit(solution)/shard_map/psum | solution.py:33
  278.5 2.2 multiply_reduce_fusion.2
  282.4 7.0 %all-to-all-start.3 = ((bf16[8,16,1024]{2,1,0:T(8,128)(2,1)}), bf16[8,16,1024]{2,1,0:T(8,128)(2,1)S(1)}, u32[]{:S(2)}, u32[]{:S(2)}) async-start(bf16[8,16,1024]{2,1,0:T(8,128)(2,1)} %bitcast.33), calls=%async_computation.3 | async-start | bytes 524288 | tf_op jit(solution)/shard_map/all_to_all | solution.py:84
  290.9 4.9 %all-to-all-done.3 = bf16[8,16,1024]{2,1,0:T(8,128)(2,1)S(1)} async-done(((bf16[8,16,1024]{2,1,0:T(8,128)(2,1)}), bf16[8,16,1024]{2,1,0:T(8,128)(2,1)S(1)}, u32[]{:S(2)}, u32[]{:S(2)}) %all-to-all-start.3) | async-done | bytes 262176 | tf_op jit(solution)/shard_map/all_to_all | solution.py:84
  297.4 6.1 %ragged-dot-none.2 = f32[128,896]{1,0:T(8,128)} custom-call(s32[1]{0:T(128)} %get-tuple-element.25, s32[2]{0:T(128)} %get-tuple-element.26, s32[1]{0:T(128)} %get-tuple-element.27, s32[1]{0:T(128)} %get-tuple-element.28, s32[1]{0:T(128)} %get-tuple-element.25, bf16[128,1024]{1,0:T(8,128)(2,1)} %broadcast_select_fusion.1, bf16[1,1024,896]{2,1,0:T(8,128)(2,1)} %get-tuple-element.69), custom_call_target="tpu_custom_call" | custom-call | flops 234881024 | bytes 2555908 | tf_op jit(solution)/shard_map/ragged_dot_general/ragged-dot-none
  303.5 6.1 %ragged-dot-none.1 = f32[128,896]{1,0:T(8,128)} custom-call(s32[1]{0:T(128)} %get-tuple-element.25, s32[2]{0:T(128)} %get-tuple-element.26, s32[1]{0:T(128)} %get-tuple-element.27, s32[1]{0:T(128)} %get-tuple-element.28, s32[1]{0:T(128)} %get-tuple-element.25, bf16[128,1024]{1,0:T(8,128)(2,1)} %broadcast_select_fusion.1, bf16[1,1024,896]{2,1,0:T(8,128)(2,1)} %get-tuple-element.71), custom_call_target="tpu_custom_call" | custom-call | flops 234881024 | bytes 2555908 | tf_op jit(solution)/shard_map/ragged_dot_general/ragged-dot-none
  309.6 2.0 multiply_convert_fusion
  311.6 6.2 %ragged-dot-none = f32[128,1024]{1,0:T(8,128)} custom-call(s32[1]{0:T(128)} %get-tuple-element.25, s32[2]{0:T(128)} %get-tuple-element.26, s32[1]{0:T(128)} %get-tuple-element.27, s32[1]{0:T(128)} %get-tuple-element.28, s32[1]{0:T(128)} %get-tuple-element.25, bf16[128,896]{1,0:T(8,128)(2,1)} %multiply_convert_fusion, bf16[1,896,1024]{2,1,0:T(8,128)(2,1)} %get-tuple-element.67), custom_call_target="tpu_custom_call" | custom-call | flops 234881024 | bytes 2588676 | tf_op jit(solution)/shard_map/ragged_dot_general/ragged-dot-none
  317.8 17.8 %all-reduce.9 = bf16[128,1024]{1,0:T(8,128)(2,1)S(1)} all-reduce(f32[128,1024]{1,0:T(8,128)} %ragged-dot-none), channel_id=1, replica_groups=mesh['dp'=1,'pool'=4,'ep'=8] {'pool'}, use_global_device_ids=true, to_apply=%region_28.33 | all-reduce | flops 131072 | bytes 786432 | tf_op jit(solution)/shard_map/psum | solution.py:51
  337.3 8.5 %all-to-all-start.5 = ((bf16[8,16,1024]{2,1,0:T(8,128)(2,1)}), bf16[8,16,1024]{2,1,0:T(8,128)(2,1)S(1)}, u32[]{:S(2)}, u32[]{:S(2)}) async-start(bf16[8,16,1024]{2,1,0:T(8,128)(2,1)} %bitcast.38), calls=%async_computation.5 | async-start | bytes 524288 | tf_op jit(solution)/shard_map/all_to_all | solution.py:87
  345.9 6.3 %all-to-all-done.5 = bf16[8,16,1024]{2,1,0:T(8,128)(2,1)S(1)} async-done(((bf16[8,16,1024]{2,1,0:T(8,128)(2,1)}), bf16[8,16,1024]{2,1,0:T(8,128)(2,1)S(1)}, u32[]{:S(2)}, u32[]{:S(2)}) %all-to-all-start.5) | async-done | bytes 262176 | tf_op jit(solution)/shard_map/all_to_all | solution.py:87
  (155 shorter events, 36.6 us)
Async XLA Ops:
  6.5 131.5 %all-reduce.5.cloned.1.call-start = ((), (), s32[]{:S(2)}) async-start(), calls=%async_computation.6 | async-start | bytes 524288 | tf_op jit(solution)/shard_map/psum | solution.py:33
  9.9 14.2 %copy-start.5 = (s32[64]{0:T(128)S(1)}, s32[64]{0:T(128)}, u32[]{:S(2)}) copy-start(s32[64]{0:T(128)} %param.24) | copy-start | bytes 772
  24.1 22.5 %copy-start.2 = (bf16[64,1024]{1,0:T(8,128)(2,1)S(1)}, bf16[64,1024]{1,0:T(8,128)(2,1)}, u32[]{:S(2)}) copy-start(bf16[64,1024]{1,0:T(8,128)(2,1)} %param.21) | copy-start | bytes 393220
  24.1 22.5 %copy-start.7 = (bf16[2,1024,256]{2,1,0:T(8,128)(2,1)S(1)}, bf16[2,1024,256]{2,1,0:T(8,128)(2,1)}, u32[]{:S(2)}) copy-start(bf16[2,1024,256]{2,1,0:T(8,128)(2,1)} %param.26) | copy-start | bytes 3145732
  61.2 2.1 copy-start.4
  61.2 36.1 %copy-start.6 = (bf16[2,1024,256]{2,1,0:T(8,128)(2,1)S(1)}, bf16[2,1024,256]{2,1,0:T(8,128)(2,1)}, u32[]{:S(2)}) copy-start(bf16[2,1024,256]{2,1,0:T(8,128)(2,1)} %param.27) | copy-start | bytes 3145732
  68.0 42.1 %all-to-all-start.1 = ((s32[8,16,1]{1,2,0:T(1,128)}), s32[8,16,1]{1,2,0:T(1,128)S(1)}, u32[]{:S(2)}, u32[]{:S(2)}) async-start(s32[8,16,1]{1,2,0:T(1,128)} %bitcast.11), calls=%async_computation.1 | async-start | bytes 8192 | tf_op jit(solution)/shard_map/all_to_all | solution.py:85
  97.6 4.4 %copy-start = (bf16[2,1,1024,896]{3,2,1,0:T(8,128)(2,1)S(1)}, bf16[2,1,1024,896]{3,2,1,0:T(8,128)(2,1)}, u32[]{:S(2)}) copy-start(bf16[2,1,1024,896]{3,2,1,0:T(8,128)(2,1)} %param.32) | copy-start | bytes 11010052
  102.0 3.4 copy-start.1
  110.1 14.4 %all-to-all-start.4 = ((s32[8,16,1]{1,2,0:T(1,128)}), s32[8,16,1]{1,2,0:T(1,128)S(1)}, u32[]{:S(2)}, u32[]{:S(2)}) async-start(s32[8,16,1]{1,2,0:T(1,128)} %bitcast.31), calls=%async_computation.4 | async-start | bytes 8192 | tf_op jit(solution)/shard_map/all_to_all | solution.py:85
  134.3 13.9 %copy-start.3 = (f32[2,1024,8]{1,2,0:T(8,128)S(1)}, f32[2,1024,8]{1,2,0:T(8,128)}, u32[]{:S(2)}) copy-start(f32[2,1024,8]{1,2,0:T(8,128)} %param.29) | copy-start | bytes 196612
  143.4 11.1 %all-to-all-start = ((bf16[8,16,1024]{2,1,0:T(8,128)(2,1)}), bf16[8,16,1024]{2,1,0:T(8,128)(2,1)S(1)}, u32[]{:S(2)}, u32[]{:S(2)}) async-start(bf16[8,16,1024]{2,1,0:T(8,128)(2,1)} %bitcast.13), calls=%async_computation | async-start | bytes 524288 | tf_op jit(solution)/shard_map/all_to_all | solution.py:84
  195.8 15.2 %all-to-all-start.2 = ((bf16[8,16,1024]{2,1,0:T(8,128)(2,1)}), bf16[8,16,1024]{2,1,0:T(8,128)(2,1)S(1)}, u32[]{:S(2)}, u32[]{:S(2)}) async-start(bf16[8,16,1024]{2,1,0:T(8,128)(2,1)} %bitcast.18), calls=%async_computation.2 | async-start | bytes 524288 | tf_op jit(solution)/shard_map/all_to_all | solution.py:87
  204.7 72.4 %all-reduce.7.cloned.1.call-start = ((), (), s32[]{:S(2)}) async-start(), calls=%async_computation.7 | async-start | bytes 524288 | tf_op jit(solution)/shard_map/psum | solution.py:33
  282.4 13.3 %all-to-all-start.3 = ((bf16[8,16,1024]{2,1,0:T(8,128)(2,1)}), bf16[8,16,1024]{2,1,0:T(8,128)(2,1)S(1)}, u32[]{:S(2)}, u32[]{:S(2)}) async-start(bf16[8,16,1024]{2,1,0:T(8,128)(2,1)} %bitcast.33), calls=%async_computation.3 | async-start | bytes 524288 | tf_op jit(solution)/shard_map/all_to_all | solution.py:84
  337.3 14.9 %all-to-all-start.5 = ((bf16[8,16,1024]{2,1,0:T(8,128)(2,1)}), bf16[8,16,1024]{2,1,0:T(8,128)(2,1)S(1)}, u32[]{:S(2)}, u32[]{:S(2)}) async-start(bf16[8,16,1024]{2,1,0:T(8,128)(2,1)} %bitcast.38), calls=%async_computation.5 | async-start | bytes 524288 | tf_op jit(solution)/shard_map/all_to_all | solution.py:87
Sparse Core Ops, SparseCore 0:
  63.4 38.3 all-reduce.4
  240.3 36.7 all-reduce.6
where the time goes:
time: 363 us; the launch traced here: 362 us
  blocking collectives  88.9 us (24%)
  local copies, waits for them, and re-layouts  54.2 us (15%)
  starting transfers between devices  46.1 us (13%)
  waiting for transfers between devices  45.9 us (13%)
  other arithmetic  43.3 us (12%)
  Pallas kernels  38.6 us (11%)
  matrix products  30.6 us (8%)
  between operations  14.2 us (4%)
    another operation x6, Pallas kernels  36.2 us
    psum x2, blocking collectives, expert_math(): return lax.psum(part_out, 'pool').astype(jnp.bfloat16)  36.1 us
    pmax x2, blocking collectives, attention_block(): lax.pmax(jnp.max(score_vals, axis=-1), 'pool')  28.2 us
    psum x2, blocking collectives, attention_block(): denom_sum = lax.psum(jnp.sum(prob_vals, axis=-1), 'pool') + new_prob  24.7 us
    psum x2, waiting for transfers between devices, attention_block(): lax.psum(jnp.einsum('tgqs,tsgd->tgqd', prob_vals.astype(jnp.bfloat16), v_...  23.5 us
    all_to_all x2, starting transfers between devices, body(): back_rows = lax.all_to_all(expert_rows, 'ep', 0, 0, tiled=True)  17.3 us
    all_to_all x2, starting transfers between devices, body(): recv_ids = lax.all_to_all(send_ids, 'ep', 0, 0, tiled=True)  16.9 us
    slice x1, local copies, waits for them, and re-layouts, body(): k_cache[layer_idx]  14.1 us
  transfers between devices with their start and end apart: 8, of which 5 were waited for; matrix products, arithmetic and copies ran while one was open for 12% of the time, Pallas kernels for 1%

commit v1 on v0

v1 whole, which is shorter than its diff:
```python
import functools

import jax
import jax.numpy as jnp
from jax import lax
from jax.experimental import pallas as pl
from jax.experimental.pallas import tpu as pltpu
from jax.sharding import PartitionSpec as P

MESH = pl.DeviceIdType.MESH
NORM_EPS = 1e-6
NEG = -1e30
BF = jnp.bfloat16
F32 = jnp.float32
NT = (((1,), (1,)), ((), ()))


def rms_norm(v):
    return v * lax.rsqrt(jnp.mean(v * v, axis=-1, keepdims=True) + NORM_EPS)


def dot(a, b):
    return jnp.dot(a, b, preferred_element_type=F32)


def layers_kernel(dims, len_ref, x_hbm, ids_ref, k_hbm, v_hbm, wq_hbm, wk_hbm, wv_hbm, wo_hbm, wr_ref,
                  w1_hbm, w3_hbm, w2_hbm, out_ref,
                  xb, xs, wqkv, kbuf, vbuf, wob, w1b, w3b, w2b, qrows, kvs, kx, vx, zst, msg, arx, orow, oag,
                  a_s, uperm, xin, act, ysend, yrecv, ybf, yret, dmat, rmat, wr3,
                  ld_sem, kv_sem, att_s, att_r, og_s, og_r, dis_s, dis_r, ys_s, ys_r, ret_s, ret_r):
    L, T, D, S, G, HD, NH, NP, NE, TC, K, FF = dims
    QG = NH // G
    SLOTS = T * K
    RE = SLOTS // NE
    CB = D // NP
    ROWS = TC * NH
    SG = S * G
    QW = NH * HD
    KW = G * HD
    scale = HD ** -0.5
    p = lax.axis_index("pool")
    e = lax.axis_index("ep")

    def pool_of(d):
        return lax.rem(p + d, NP)

    def ep_of(d):
        return lax.rem(e + d, NE)

    barrier = pltpu.get_barrier_semaphore()
    for dp_ in range(NP):
        for de in range(NE):
            if dp_ or de:
                pl.semaphore_signal(barrier, inc=1, device_id={"pool": pool_of(dp_), "ep": ep_of(de)},
                                    device_id_type=MESH)

    def qkv_copies(l):
        return [pltpu.make_async_copy(wq_hbm.at[l], wqkv.at[:, pl.ds(0, QW)], ld_sem.at[0]),
                pltpu.make_async_copy(wk_hbm.at[l], wqkv.at[:, pl.ds(QW, KW)], ld_sem.at[1]),
                pltpu.make_async_copy(wv_hbm.at[l], wqkv.at[:, pl.ds(QW + KW, KW)], ld_sem.at[2])]

    def kv_copies(l, i):
        c = pool_of(i + 1)
        tok = pl.ds(pl.multiple_of(c * TC, TC), TC)
        return [pltpu.make_async_copy(k_hbm.at[l, tok], kbuf.at[i], kv_sem.at[0, i]),
                pltpu.make_async_copy(v_hbm.at[l, tok], vbuf.at[i], kv_sem.at[1, i])]

    def wo_copies(l):
        return [pltpu.make_async_copy(wo_hbm.at[l], wob, ld_sem.at[3])]

    def up_copies(l):
        return [pltpu.make_async_copy(w1_hbm.at[l, 0], w1b, ld_sem.at[4]),
                pltpu.make_async_copy(w3_hbm.at[l, 0], w3b, ld_sem.at[5])]

    def down_copies(l):
        return [pltpu.make_async_copy(w2_hbm.at[l, 0, :, pl.ds(q * CB, CB)], w2b.at[q], ld_sem.at[6 + q])
                for q in range(NP)]

    def start(copies):
        for c in copies:
            c.start()

    def wait(copies):
        for c in copies:
            c.wait()

    xcopy = pltpu.make_async_copy(x_hbm, xb, ld_sem.at[6 + NP])
    xcopy.start()
    start(qkv_copies(0))
    for i in range(NP):
        start(kv_copies(0, i))
    start(wo_copies(0))
    start(up_copies(0))
    start(down_copies(0))

    slot_col = lax.broadcasted_iota(jnp.int32, (SLOTS, SLOTS), 0)
    pair_row = lax.broadcasted_iota(jnp.int32, (SLOTS, SLOTS), 1)
    upper = (slot_col < pair_row).astype(F32).astype(BF)
    want_rank = lax.rem(slot_col, RE).astype(F32)
    for l in range(L):
        idrow = jnp.concatenate([ids_ref[l, k:k + 1, :] for k in range(K)], axis=1)
        same = (jnp.broadcast_to(idrow, (SLOTS, SLOTS)) == lax.div(slot_col, RE))
        rank = dot(same.astype(F32).astype(BF), upper)
        pick = jnp.where(jnp.logical_and(same, rank == want_rank), 1.0, 0.0).astype(F32)
        rmat[l] = pick.T.astype(BF)
        tot = pick[:, 0:T]
        for k in range(1, K):
            tot = tot + pick[:, k * T:(k + 1) * T]
        dmat[l] = tot.astype(BF)
        wr = wr_ref[l]
        hi = wr.astype(BF).astype(F32)
        mid = (wr - hi).astype(BF).astype(F32)
        lo = wr - hi - mid
        wr3[l] = jnp.concatenate([hi, mid, lo, jnp.zeros_like(lo)], axis=0).astype(BF)

    hrow = lax.broadcasted_iota(jnp.int32, (NH, SG), 0)
    pcol = lax.broadcasted_iota(jnp.int32, (NH, SG), 1)
    posm = jnp.where(lax.rem(pcol, G) == lax.div(hrow, QG), lax.div(pcol, G), jnp.int32(1 << 30))
    lane = lax.broadcasted_iota(jnp.int32, (NH, HD), 1)
    ecol = lax.broadcasted_iota(jnp.int32, (wr_ref.shape[1], T), 0)

    xcopy.wait()
    xs[...] = xb[...].astype(F32)

    def layer(l, carry):
        more = l + 1 < L
        wait(qkv_copies(l))
        hn = rms_norm(xs[...]).astype(BF)
        for b in range((QW + 2 * KW) // (2 * HD)):
            r = dot(hn, wqkv[:, b * 2 * HD:(b + 1) * 2 * HD]).astype(BF).astype(F32)
            if b * 2 * HD < QW:
                for j in range(2):
                    qrows[pl.ds(2 * b + j, T, stride=NH), :] = r[:, j * HD:(j + 1) * HD]
            else:
                kvs[:, b * 2 * HD - QW:(b + 1) * 2 * HD - QW] = r

        @pl.when(more)
        def _():
            start(qkv_copies(l + 1))

        own_tok = pl.ds(pl.multiple_of(p * TC, TC), TC)
        for h in range(NH):
            g = h // QG
            kx[pl.ds(h, TC, stride=NH), :] = kvs[own_tok, g * HD:(g + 1) * HD]
            vx[pl.ds(h, TC, stride=NH), :] = kvs[own_tok, KW + g * HD:KW + (g + 1) * HD]

        @pl.when(l == 0)
        def _():
            pl.semaphore_wait(barrier, NP * NE - 1)

        def att_send(i):
            return pltpu.make_async_remote_copy(
                src_ref=msg.at[l, i], dst_ref=arx.at[l, i], send_sem=att_s.at[l, i], recv_sem=att_r.at[l, i],
                device_id={"pool": pool_of(i + 1), "ep": e}, device_id_type=MESH)

        def chunk(i, c2):
            c = pool_of(i + 1)
            wait(kv_copies(l, i))
            for j0 in range(0, TC, 8):
                sc = []
                for j in range(j0, j0 + 8):
                    t = c * TC + j
                    qt = qrows[pl.ds(pl.multiple_of(t * NH, NH), NH), :].astype(BF)
                    s = lax.dot_general(qt, kbuf[i, j], NT, preferred_element_type=F32) * scale
                    sc.append(jnp.where(posm < len_ref[t] - p * S, s, NEG))
                mx = [jnp.max(s, axis=1, keepdims=True) for s in sc]
                pr = [jnp.exp(s - m) for s, m in zip(sc, mx)]
                ls = [jnp.sum(q, axis=1, keepdims=True) for q in pr]
                for n, j in enumerate(range(j0, j0 + 8)):
                    msg[l, i, j * NH:(j + 1) * NH, :] = dot(pr[n].astype(BF), vbuf[i, j])
                    zst[j * NH:(j + 1) * NH, :] = jnp.where(lane == 0, mx[n], ls[n])
            msg[l, i, ROWS:ROWS + 8, :] = zst[...].T[0:8, :]

            @pl.when(i < NP - 1)
            def _():
                att_send(i).start()

            @pl.when(more)
            def _():
                start(kv_copies(l + 1, i))

            return c2

        lax.fori_loop(0, NP, chunk, 0)

        q_own = qrows[pl.ds(pl.multiple_of(p * ROWS, ROWS), ROWS), :]
        s_new = jnp.sum(q_own * kx[...], axis=1, keepdims=True) * scale
        for i in range(NP - 1):
            att_send(i).wait_recv()
            zst[8 * i:8 * i + 8, :] = arx[l, i, ROWS:ROWS + 8, :]
        zst[8 * (NP - 1):8 * NP, :] = msg[l, NP - 1, ROWS:ROWS + 8, :]
        zc = zst[...].T
        ms = [zc[:, 8 * i:8 * i + 1] for i in range(NP)]
        top = s_new
        for m in ms:
            top = jnp.maximum(top, m)
        p_new = jnp.exp(s_new - top)
        den = p_new
        num = p_new * vx[...]
        for i in range(NP):
            w = jnp.exp(ms[i] - top)
            den = den + w * zc[:, 8 * i + 1:8 * i + 2]
            num = num + w * (arx[l, i, 0:ROWS, :] if i < NP - 1 else msg[l, i, 0:ROWS, :])
        orow[...] = num / den
        for h in range(NH):
            oag[l, own_tok, h * HD:(h + 1) * HD] = orow[pl.ds(h, TC, stride=NH), :].astype(BF)

        def og_send(d):
            return pltpu.make_async_remote_copy(
                src_ref=oag.at[l, own_tok], dst_ref=oag.at[l, own_tok], send_sem=og_s.at[l, d - 1],
                recv_sem=og_r.at[l, d - 1], device_id={"pool": pool_of(d), "ep": e}, device_id_type=MESH)

        for d in range(1, NP):
            og_send(d).start()
        wait(wo_copies(l))
        for d in range(1, NP):
            og_send(d).wait_recv()

        for b in range(NP):
            cols = slice(b * CB, (b + 1) * CB)
            a_s[:, cols] = (xs[:, cols] + dot(oag[l], wob[:, cols])).astype(BF).astype(F32)

        @pl.when(more)
        def _():
            start(wo_copies(l + 1))

        u = rms_norm(a_s[...]).astype(BF)
        for b in range(NP):
            cols = slice(b * CB, (b + 1) * CB)
            uperm[l, :, cols] = dot(dmat[l], u[:, cols]).astype(BF)

        def dis_send(d):
            dst = ep_of(d)
            return pltpu.make_async_remote_copy(
                src_ref=uperm.at[l, pl.ds(pl.multiple_of(dst * RE, RE), RE)],
                dst_ref=xin.at[l, pl.ds(pl.multiple_of(e * RE, RE), RE)],
                send_sem=dis_s.at[l, d - 1], recv_sem=dis_r.at[l, d - 1],
                device_id={"pool": p, "ep": dst}, device_id_type=MESH)

        for d in range(1, NE):
            dis_send(d).start()
        mine = pl.ds(pl.multiple_of(e * RE, RE), RE)
        xin[l, mine, :] = uperm[l, mine, :]

        lg3 = lax.dot_general(wr3[l], u, NT, preferred_element_type=F32)
        ne = wr_ref.shape[1]
        lg = lg3[0:ne] + lg3[ne:2 * ne] + lg3[2 * ne:3 * ne]
        picked = [jnp.sum(jnp.where(ecol == ids_ref[l, k:k + 1, :], lg, 0.0), axis=0, keepdims=True)
                  for k in range(K)]
        gtop = picked[0]
        for k in range(1, K):
            gtop = jnp.maximum(gtop, picked[k])
        ex = [jnp.exp(v - gtop) for v in picked]
        tot = ex[0]
        for k in range(1, K):
            tot = tot + ex[k]
        grow = jnp.concatenate([v / tot for v in ex], axis=1)
        gcol = jnp.broadcast_to(grow, (SLOTS, SLOTS)).T[:, 0:1]

        wait(up_copies(l))
        for d in range(1, NE):
            dis_send(d).wait_recv()

        xe = xin[l]
        f0 = 0
        while f0 < FF:
            fw = min(2 * HD, FF - f0)
            h1 = dot(xe, w1b[:, f0:f0 + fw])
            h3 = dot(xe, w3b[:, f0:f0 + fw])
            act[:, f0:f0 + fw] = (h1 * jax.nn.sigmoid(h1) * h3).astype(BF)
            f0 += fw

        @pl.when(more)
        def _():
            start(up_copies(l + 1))

        def ys_send(d):
            return pltpu.make_async_remote_copy(
                src_ref=ysend.at[l, d - 1], dst_ref=yrecv.at[l, d - 1], send_sem=ys_s.at[l, d - 1],
                recv_sem=ys_r.at[l, d - 1], device_id={"pool": pool_of(d), "ep": e}, device_id_type=MESH)

        wait(down_copies(l))
        for d in (2, 1, 3, 0) if NP == 4 else list(range(1, NP)) + [0]:
            ysend[l, (d - 1) % NP] = dot(act[...], w2b[pool_of(d)])
            if d:
                ys_send(d).start()

        @pl.when(more)
        def _():
            start(down_copies(l + 1))

        acc = ysend[l, NP - 1]
        for d in range(1, NP):
            ys_send(d).wait_recv()
            acc = acc + yrecv[l, d - 1]
        ybf[l] = acc.astype(BF)

        def ret_send(dp_, de):
            dst = ep_of(de)
            return pltpu.make_async_remote_copy(
                src_ref=ybf.at[l, pl.ds(pl.multiple_of(dst * RE, RE), RE)],
                dst_ref=yret.at[l, p, pl.ds(pl.multiple_of(e * RE, RE), RE)],
                send_sem=ret_s.at[l, dp_ * NE + de], recv_sem=ret_r.at[l, dp_ * NE + de],
                device_id={"pool": pool_of(dp_), "ep": dst}, device_id_type=MESH)

        others = [(a, b) for a in range(NP) for b in range(NE) if a or b]
        for a, b in others:
            ret_send(a, b).start()
        yret[l, p, mine, :] = ybf[l, mine, :]
        for a, b in others:
            ret_send(a, b).wait_recv()

        for b in range(NP):
            cols = slice(b * CB, (b + 1) * CB)
            yp = dot(rmat[l], yret[l, b]) * gcol
            mixed = yp[0:T]
            for k in range(1, K):
                mixed = mixed + yp[k * T:(k + 1) * T]
            xs[:, cols] = (a_s[:, cols] + mixed).astype(BF).astype(F32)

        for i in range(NP - 1):
            att_send(i).wait_send()
            og_send(i + 1).wait_send()
            ys_send(i + 1).wait_send()
        for d in range(1, NE):
            dis_send(d).wait_send()
        for a, b in others:
            ret_send(a, b).wait_send()
        return carry

    lax.fori_loop(0, L, layer, 0)
    out_ref[...] = xs[...].astype(BF)


def solution(mesh):
    tok_spec = P(("dp", "ep"), None)
    cache_spec = P(None, ("dp", "ep"), "pool", None, None)
    up_spec = P(None, "ep", None, "pool")
    down_spec = P(None, "ep", "pool", None)
    in_specs = (tok_spec, cache_spec, cache_spec, P(("dp", "ep")), P(), P(), P(), P(), P(),
                P(None, ("dp", "ep"), None), up_spec, up_spec, down_spec)
    NP, NE = mesh.shape["pool"], mesh.shape["ep"]

    def body(hidden, k_cache, v_cache, cache_len, w_q, w_k, w_v, w_o, w_router, ids, w_one, w_three, w_two):
        L = w_q.shape[0]
        T, D = hidden.shape
        S, G, HD = k_cache.shape[2:]
        NH = w_q.shape[2] // HD
        K = ids.shape[2]
        FF = w_one.shape[3]
        TC = T // NP
        SLOTS, CB, ROWS, SG = T * K, D // NP, TC * NH, S * G
        assert w_one.shape[1] == 1 and SLOTS == HD and ROWS == HD and w_router.shape[2] == 8
        dims = (L, T, D, S, G, HD, NH, NP, NE, TC, K, FF)
        kc = k_cache.reshape(L, T, SG, HD)
        vc = v_cache.reshape(L, T, SG, HD)
        wr_t = jnp.swapaxes(w_router, 1, 2)
        ids_t = jnp.swapaxes(ids, 1, 2)
        V = pltpu.VMEM
        dma = pltpu.SemaphoreType.DMA
        anyspec = pl.BlockSpec(memory_space=pl.ANY)
        vspec = pl.BlockSpec(memory_space=pltpu.VMEM)
        scratch = [
            V((T, D), BF), V((T, D), F32), V((D, (NH + 2 * G) * HD), BF),
            V((NP, TC, SG, HD), BF), V((NP, TC, SG, HD), BF), V((D, D), BF),
            V((D, FF), BF), V((D, FF), BF), V((NP, FF, CB), BF),
            V((T * NH, HD), F32), V((T, 2 * G * HD), F32), V((ROWS, HD), F32), V((ROWS, HD), F32),
            V((ROWS, HD), F32), V((L, NP, ROWS + 8, HD), F32), V((L, NP - 1, ROWS + 8, HD), F32),
            V((ROWS, HD), F32), V((L, T, NH * HD), BF),
            V((T, D), F32), V((L, SLOTS, D), BF), V((L, SLOTS, D), BF), V((SLOTS, FF), BF),
            V((L, NP, SLOTS, CB), F32), V((L, NP - 1, SLOTS, CB), F32),
            V((L, SLOTS, CB), BF), V((L, NP, SLOTS, CB), BF),
            V((L, SLOTS, T), BF), V((L, SLOTS, SLOTS), BF), V((L, 32, D), BF),
            dma((7 + NP,)), dma((2, NP)),
            dma((L, NP - 1)), dma((L, NP - 1)), dma((L, NP - 1)), dma((L, NP - 1)),
            dma((L, NE - 1)), dma((L, NE - 1)), dma((L, NP - 1)), dma((L, NP - 1)),
            dma((L, NP * NE)), dma((L, NP * NE)),
        ]
        return pl.pallas_call(
            functools.partial(layers_kernel, dims),
            out_shape=jax.ShapeDtypeStruct((T, D), BF),
            in_specs=[pl.BlockSpec(memory_space=pltpu.SMEM), anyspec, vspec, anyspec, anyspec, anyspec, anyspec,
                      anyspec, anyspec, vspec, anyspec, anyspec, anyspec],
            out_specs=vspec,
            scratch_shapes=scratch,
            name="moe_layers",
            compiler_params=pltpu.CompilerParams(collective_id=0, has_side_effects=True,
                                                 vmem_limit_bytes=60 * 1024 * 1024),
        )(cache_len, hidden, ids_t, kc, vc, w_q, w_k, w_v, w_o, wr_t, w_one, w_three, w_two)

    return jax.shard_map(body, mesh=mesh, in_specs=in_specs, out_specs=tok_spec, check_vma=False)
```

time: 363 us -> 81.2 us (0.22)
  blocking collectives: 88.9 us -> 0 us
  local copies, waits for them, and re-layouts: 54.2 us -> 1.57 us
  starting transfers between devices: 46.1 us -> 0 us
  waiting for transfers between devices: 45.9 us -> 0 us
  other arithmetic: 43.3 us -> 0 us
  Pallas kernels: 38.6 us -> 79.5 us
  matrix products: 30.6 us -> 0 us
  between operations: 14.2 us -> 0.01 us
    pallas_call x0 -> x1, Pallas kernels: none -> 79.5 us  [body(): pl.pallas_call(functools.partial(layers_kernel, dims), out_shape=jax.Shap...]
    psum x4 -> x0, blocking collectives: 60.7 us -> none  [the longest x2 36.1 us: expert_math(): return lax.psum(part_out, 'pool').astype(jnp.bfloat16)]
    all_to_all x6 -> x0, starting transfers between devices: 46.1 us -> none  [the longest x2 17.3 us: body(): back_rows = lax.all_to_all(expert_rows, 'ep', 0, 0, tiled=True)]
    another operation x6 -> x0, Pallas kernels: 36.2 us -> none
    dot_general x16 -> x0, matrix products: 30.6 us -> none  [the longest x2 11.7 us: attention_block(): jnp.einsum('tgqd,tsgd->tgqs', query, k_rows, preferred_element_type=jnp.f...]
    slice x5 -> x0, local copies, waits for them, and re-layouts: 28.3 us -> none  [the longest x1 14.1 us: body(): k_cache[layer_idx]]
    pmax x2 -> x0, blocking collectives: 28.2 us -> none  [attention_block(): lax.pmax(jnp.max(score_vals, axis=-1), 'pool')]
    psum x2 -> x0, waiting for transfers between devices: 23.5 us -> none  [attention_block(): lax.psum(jnp.einsum('tgqs,tsgd->tgqd', prob_vals.astype(jnp.bfloat16), v_...]
  transfers between devices with their start and end apart: 8 -> 0, of which waited for: 5 -> 0; matrix products, arithmetic and copies ran while one was open for 12% -> 0% of each run, Pallas kernels for 1% -> 0%
where the time goes in v1:
time: 81.2 us; the launch traced here: 81.1 us
  Pallas kernels  79.5 us (98%)
  local copies, waits for them, and re-layouts  1.57 us (2%)
    pallas_call x1, Pallas kernels, body(): pl.pallas_call(functools.partial(layers_kernel, dims), out_shape=jax.Shap...  79.5 us

profile of v1, /device:TPU:97, one launch (start us, length us, event | category | flops | bytes accessed | tf_op | source)
XLA Modules:
  0.0 81.1 jit_solution(16141117569387574964)
XLA Ops:
  0.0 79.5 %moe_layers.1 = bf16[64,1024]{1,0:T(8,128)(2,1)} custom-call(s32[64]{0:T(128)} %len_ref.1, bf16[64,1024]{1,0:T(8,128)(2,1)} %x_hbm.1, s32[2,2,64]{2,1,0:T(2,128)} %bitcast.7, bf16[2,64,512,128]{3,2,1,0:T(8,128)(2,1)} %bitcast.4, bf16[2,64,512,128]{3,2,1,0:T(8,128)(2,1)} %bitcast.5, bf16[2,1024,1024]{2,1,0:T(8,128)(2,1)} %wq_hbm.1, ...), custom_call_target="tpu_custom_call" | custom-call | tf_op jit(solution)/shard_map/moe_layers/pallas_call | solution.py:379
  79.5 1.6 %copy.15 = bf16[64,1024]{1,0:T(8,128)(2,1)} copy(bf16[64,1024]{1,0:T(8,128)(2,1)} %moe_layers.1) | data formatting | bytes 262144

commit v2 on v0

v2 whole, which is shorter than its diff:
```python
import functools

import jax
import jax.numpy as jnp
from jax import lax
from jax.experimental import pallas as pl
from jax.experimental.pallas import tpu as pltpu
from jax.sharding import PartitionSpec as P

MESH = pl.DeviceIdType.MESH
NORM_EPS = 1e-6
NEG = -1e30
BF = jnp.bfloat16
F32 = jnp.float32
NT = (((1,), (1,)), ((), ()))


def rms_norm(v):
    return v * lax.rsqrt(jnp.mean(v * v, axis=-1, keepdims=True) + NORM_EPS)


def dot(a, b):
    return jnp.dot(a, b, preferred_element_type=F32)


def layers_kernel(dims, len_ref, x_hbm, ids_hbm, k_hbm, v_hbm, wq_hbm, wk_hbm, wv_hbm, wo_hbm, wr_hbm,
                  w1_hbm, w3_hbm, w2_hbm, out_ref,
                  xb, xs, idb, wrb, wqkv, kbuf, vbuf, wob, w1b, w3b, w2b, qrows, kvs, kx, vx, zst, msg, arx, orow, oag,
                  a_s, uperm, xin, act, ys, ysum, rlr, drr, srr, ybf, yret,
                  ld_sem, kv_sem, att_s, att_r, og_s, og_r, dis_s, dis_r, rl_s, rl_r, dr_s, dr_r, sr_s, sr_r,
                  ret_s, ret_r):
    L, T, D, S, G, HD, NH, NP, NE, TC, K, FF = dims
    QG = NH // G
    SLOTS = T * K
    RE = SLOTS // NE
    CB = D // NP
    SG = S * G
    QW = NH * HD
    KW = G * HD
    TU = TC // 2
    TH = T // 2
    UR = TU * NH
    NU = 2 * NP
    NX = NE // 2
    RG = SLOTS // 2
    RH = RG // 2
    BW = 2 * HD
    scale = HD ** -0.5
    p = lax.axis_index("pool")
    e = lax.axis_index("ep")
    chip = lax.div(e, 2)
    core = lax.rem(e, 2)

    def pool_of(d):
        return lax.rem(p + d, NP)

    rel = [(0, 0), (0, 1), (1, 0), (NX - 1, 0), (1, 1), (NX - 1, 1)]
    rel += [(dx, dc) for dx in range(2, NX - 1) for dc in range(2)]
    NR = len(rel)

    def ep_sender(r):
        return lax.rem(chip + rel[r][0], NX) * 2 + lax.rem(core + rel[r][1], 2)

    def ep_receiver(r):
        return lax.rem(chip + NX - rel[r][0], NX) * 2 + lax.rem(core + rel[r][1], 2)

    barrier = pltpu.get_barrier_semaphore()
    for dp_ in range(NP):
        for de in range(NE):
            if dp_ or de:
                pl.semaphore_signal(barrier, inc=1,
                                    device_id={"pool": pool_of(dp_), "ep": lax.rem(e + de, NE)},
                                    device_id_type=MESH)

    def block(ref, l, b, n):
        return ref.at[l, :, pl.ds(b * BW, n)]

    def qkv_copies(l):
        out = [pltpu.make_async_copy(block(wq_hbm, l, b, BW), wqkv.at[b], ld_sem.at[b]) for b in range(QW // BW)]
        n = QW // BW
        out.append(pltpu.make_async_copy(wk_hbm.at[l], wqkv.at[n], ld_sem.at[n]))
        out.append(pltpu.make_async_copy(wv_hbm.at[l], wqkv.at[n + 1], ld_sem.at[n + 1]))
        return out

    s0 = QW // BW + 2

    def kv_copies(l, n):
        half, i = divmod(n, NP) if isinstance(n, int) else (lax.div(n, NP), lax.rem(n, NP))
        tok = pl.ds(pl.multiple_of(half * TH + lax.rem(p + i + 1, NP) * TU, TU), TU)
        return [pltpu.make_async_copy(k_hbm.at[l, tok], kbuf.at[n], kv_sem.at[0, n]),
                pltpu.make_async_copy(v_hbm.at[l, tok], vbuf.at[n], kv_sem.at[1, n])]

    def wo_copies(l):
        return [pltpu.make_async_copy(wo_hbm.at[l], wob, ld_sem.at[s0])]

    def up_copies(l):
        return [pltpu.make_async_copy(w1_hbm.at[l, 0], w1b, ld_sem.at[s0 + 1]),
                pltpu.make_async_copy(w3_hbm.at[l, 0], w3b, ld_sem.at[s0 + 2])]

    def down_copies(l):
        return [pltpu.make_async_copy(w2_hbm.at[l, 0, :, pl.ds(q * CB, CB)], w2b.at[q], ld_sem.at[s0 + 3 + q])
                for q in range(NP)]

    def start(copies):
        for c in copies:
            c.start()

    def wait(copies):
        for c in copies:
            c.wait()

    small = [pltpu.make_async_copy(x_hbm, xb, ld_sem.at[s0 + 3 + NP]),
             pltpu.make_async_copy(ids_hbm, idb, ld_sem.at[s0 + 4 + NP]),
             pltpu.make_async_copy(wr_hbm, wrb, ld_sem.at[s0 + 5 + NP])]
    small[0].start()
    start(qkv_copies(0))
    start(small[1:])
    for n in range(2):
        start(kv_copies(0, n))

    hrow = lax.broadcasted_iota(jnp.int32, (NH, SG), 0)
    pcol = lax.broadcasted_iota(jnp.int32, (NH, SG), 1)
    posm = jnp.where(lax.rem(pcol, G) == lax.div(hrow, QG), lax.div(pcol, G), jnp.int32(1 << 30))
    lane = lax.broadcasted_iota(jnp.int32, (NH, HD), 1)
    NEX = wrb.shape[1]
    ecol = lax.broadcasted_iota(jnp.int32, (NEX, T), 0)

    small[0].wait()
    xs[...] = xb[...].astype(F32)
    wait(small[1:])

    def layer(l, carry):
        more = l + 1 < L
        first = l == 0

        def att_send(half, i):
            return pltpu.make_async_remote_copy(
                src_ref=msg.at[l, half, i], dst_ref=arx.at[l, half, i], send_sem=att_s.at[l, half, i],
                recv_sem=att_r.at[l, half, i], device_id={"pool": pool_of(i + 1), "ep": e}, device_id_type=MESH)

        def own_tok(half):
            return pl.ds(pl.multiple_of(half * TH + p * TU, TU), TU)

        def og_send(half, d):
            return pltpu.make_async_remote_copy(
                src_ref=oag.at[l, own_tok(half)], dst_ref=oag.at[l, own_tok(half)], send_sem=og_s.at[l, half, d - 1],
                recv_sem=og_r.at[l, half, d - 1], device_id={"pool": pool_of(d), "ep": e}, device_id_type=MESH)

        def dis_send(r):
            dst = ep_receiver(r)
            return pltpu.make_async_remote_copy(
                src_ref=uperm.at[l, pl.ds(pl.multiple_of(dst * RE, RE), RE)], dst_ref=xin.at[l, pl.ds(r * RE, RE)],
                send_sem=dis_s.at[l, r], recv_sem=dis_r.at[l, r],
                device_id={"pool": p, "ep": dst}, device_id_type=MESH)

        def ring_dev(way):
            return {"pool": pool_of(1 if way == 0 else NP - 1), "ep": e}

        def relay_send(g, way):
            return pltpu.make_async_remote_copy(
                src_ref=ys.at[l, g, 2, pl.ds(way * RH, RH)], dst_ref=rlr.at[l, g, way], send_sem=rl_s.at[l, g, way],
                recv_sem=rl_r.at[l, g, way], device_id=ring_dev(way), device_id_type=MESH)

        def direct_send(g, way):
            return pltpu.make_async_remote_copy(
                src_ref=ys.at[l, g, 1 if way == 0 else 3, pl.ds((1 - way) * RH, RH)], dst_ref=drr.at[l, g, way],
                send_sem=dr_s.at[l, g, way], recv_sem=dr_r.at[l, g, way], device_id=ring_dev(way),
                device_id_type=MESH)

        def sum_send(g, way):
            return pltpu.make_async_remote_copy(
                src_ref=ysum.at[l, g, way], dst_ref=srr.at[l, g, way], send_sem=sr_s.at[l, g, way],
                recv_sem=sr_r.at[l, g, way], device_id=ring_dev(way), device_id_type=MESH)

        def ret_send(dp_, r):
            dst = ep_sender(r)
            return pltpu.make_async_remote_copy(
                src_ref=ybf.at[l, pl.ds(r * RE, RE)],
                dst_ref=yret.at[l, p, pl.ds(pl.multiple_of(e * RE, RE), RE)],
                send_sem=ret_s.at[l, dp_, r], recv_sem=ret_r.at[l, dp_, r],
                device_id={"pool": pool_of(dp_), "ep": dst}, device_id_type=MESH)

        with jax.named_scope("qkv"):
            hn = rms_norm(xs[...]).astype(BF)
            cps = qkv_copies(l)
            for b in range(len(cps)):
                cps[b].wait()
                r = dot(hn, wqkv[b]).astype(BF).astype(F32)
                if b * BW < QW:
                    for j in range(2):
                        qrows[pl.ds(2 * b + j, T, stride=NH), :] = r[:, j * HD:(j + 1) * HD]
                else:
                    kvs[:, b * BW - QW:(b + 1) * BW - QW] = r

            @pl.when(first)
            def _():
                for n in range(2, 4):
                    start(kv_copies(l, n))

            for half in range(2):
                for h in range(NH):
                    g = h // QG
                    kx[pl.ds(half * UR + h, TU, stride=NH), :] = kvs[own_tok(half), g * HD:(g + 1) * HD]
                    vx[pl.ds(half * UR + h, TU, stride=NH), :] = kvs[own_tok(half), KW + g * HD:KW + (g + 1) * HD]

        def combine(half):
            with jax.named_scope("combine"):
                orows = pl.ds(pl.multiple_of((half * TH + p * TU) * NH, UR), UR)
                hrows = pl.ds(pl.multiple_of(half * UR, UR), UR)
                s_new = jnp.sum(qrows[orows, :] * kx[hrows, :], axis=1, keepdims=True) * scale
                for i in range(NP - 1):
                    att_send(half, i).wait_recv()
                    zst[8 * i:8 * i + 8, :] = arx[l, half, i, UR:UR + 8, :]
                zst[8 * (NP - 1):8 * NP, :] = msg[l, half, NP - 1, UR:UR + 8, :]
                zc = zst[...].T
                cut = [zc[(i % 2) * UR:(i % 2) * UR + UR] for i in range(NP)]
                ms = [cut[i][:, 8 * i:8 * i + 1] for i in range(NP)]
                top = s_new
                for m in ms:
                    top = jnp.maximum(top, m)
                p_new = jnp.exp(s_new - top)
                den = p_new
                num = p_new * vx[hrows, :]
                for i in range(NP):
                    w = jnp.exp(ms[i] - top)
                    den = den + w * cut[i][:, 8 * i + 1:8 * i + 2]
                    num = num + w * (arx[l, half, i, 0:UR, :] if i < NP - 1 else msg[l, half, i, 0:UR, :])
                orow[...] = num / den
                for h in range(NH):
                    oag[l, own_tok(half), h * HD:(h + 1) * HD] = orow[pl.ds(h, TU, stride=NH), :].astype(BF)
                for d in (2, 1, 3):
                    og_send(half, d).start()

        def chunk(it, c2):
            half = lax.div(it, NP // 2)
            i0 = lax.rem(it, NP // 2) * 2
            for un in range(2):
                n = 2 * it + un
                wait(kv_copies(l, n))
                nxt = n + 4

                @pl.when(jnp.logical_and(first, nxt < NU))
                def _():
                    start(kv_copies(l, nxt))

            @pl.when(jnp.logical_and(first, it == 2))
            def _():
                start(wo_copies(l))
                start(up_copies(l))
                start(down_copies(l))

            for un in range(2):
                i = i0 + un
                n = 2 * it + un
                sc = []
                for j in range(TU):
                    t = half * TH + lax.rem(p + i + 1, NP) * TU + j
                    qt = qrows[pl.ds(pl.multiple_of(t * NH, NH), NH), :].astype(BF)
                    s = lax.dot_general(qt, kbuf[n, j], NT, preferred_element_type=F32) * scale
                    sc.append(jnp.where(posm < len_ref[t] - p * S, s, NEG))
                mx = [jnp.max(s, axis=1, keepdims=True) for s in sc]
                pr = [jnp.exp(s - m) for s, m in zip(sc, mx)]
                ls = [jnp.sum(q, axis=1, keepdims=True) for q in pr]
                for j in range(TU):
                    msg[l, half, i, j * NH:(j + 1) * NH, :] = dot(pr[j].astype(BF), vbuf[n, j])
                    zst[un * UR + j * NH:un * UR + (j + 1) * NH, :] = jnp.where(lane == 0, mx[j], ls[j])
            zt = zst[...].T[0:8, :]
            for un in range(2):
                msg[l, half, i0 + un, UR:UR + 8, :] = zt

            @pl.when(jnp.logical_and(first, it == 0))
            def _():
                pl.semaphore_wait(barrier, NP * NE - 1)

            att_send(half, i0).start()

            @pl.when(i0 == 0)
            def _():
                att_send(half, i0 + 1).start()

            @pl.when(it == 2)
            def _():
                combine(0)

            return c2

        with jax.named_scope("attn"):
            lax.fori_loop(0, NP, chunk, 0)

        @pl.when(more)
        def _():
            start(qkv_copies(l + 1))
            for n in range(NU):
                start(kv_copies(l + 1, n))

        combine(1)

        with jax.named_scope("tables"):
            slot_col = lax.broadcasted_iota(jnp.int32, (SLOTS, SLOTS), 0)
            pair_row = lax.broadcasted_iota(jnp.int32, (SLOTS, SLOTS), 1)
            upper = (slot_col < pair_row).astype(F32).astype(BF)
            want_rank = lax.rem(slot_col, RE).astype(F32)
            idrow = jnp.concatenate([idb[l, k:k + 1, :] for k in range(K)], axis=1)
            same = (jnp.broadcast_to(idrow, (SLOTS, SLOTS)) == lax.div(slot_col, RE))
            rank = dot(same.astype(F32).astype(BF), upper)
            pick = jnp.where(jnp.logical_and(same, rank == want_rank), 1.0, 0.0).astype(F32)
            rmat = pick.T.astype(BF)
            dmat = pick[:, 0:T]
            for k in range(1, K):
                dmat = dmat + pick[:, k * T:(k + 1) * T]
            dmat = dmat.astype(BF)
            wr = wrb[l]
            hi = wr.astype(BF).astype(F32)
            mid = (wr - hi).astype(BF).astype(F32)
            lo = wr - hi - mid
            wr3 = jnp.concatenate([hi, mid, lo, jnp.zeros_like(lo)], axis=0).astype(BF)

        with jax.named_scope("agwait"):
            wait(wo_copies(l))
            for half in range(2):
                for d in range(1, NP):
                    og_send(half, d).wait_recv()

        with jax.named_scope("oproj"):
            for b in range(NP):
                cols = slice(b * CB, (b + 1) * CB)
                a_s[:, cols] = (xs[:, cols] + dot(oag[l], wob[:, cols])).astype(BF).astype(F32)

            @pl.when(more)
            def _():
                start(wo_copies(l + 1))

            u = rms_norm(a_s[...]).astype(BF)
            for b in range(NP):
                cols = slice(b * CB, (b + 1) * CB)
                uperm[l, :, cols] = dot(dmat, u[:, cols]).astype(BF)
            for r in range(1, NR):
                dis_send(r).start()
            xin[l, 0:RE, :] = uperm[l, pl.ds(pl.multiple_of(e * RE, RE), RE), :]

        with jax.named_scope("gates"):
            lg3 = lax.dot_general(wr3, u, NT, preferred_element_type=F32)
            lg = lg3[0:NEX] + lg3[NEX:2 * NEX] + lg3[2 * NEX:3 * NEX]
            picked = [jnp.sum(jnp.where(ecol == idb[l, k:k + 1, :], lg, 0.0), axis=0, keepdims=True)
                      for k in range(K)]
            gtop = picked[0]
            for k in range(1, K):
                gtop = jnp.maximum(gtop, picked[k])
            ex = [jnp.exp(v - gtop) for v in picked]
            tot = ex[0]
            for k in range(1, K):
                tot = tot + ex[k]
            grow = jnp.concatenate([v / tot for v in ex], axis=1)
            gcol = jnp.broadcast_to(grow, (SLOTS, SLOTS)).T[:, 0:1]
            wait(up_copies(l))

        def up(g):
            for r in range(g * NR // 2, (g + 1) * NR // 2):
                if r:
                    dis_send(r).wait_recv()
            xe = xin[l, g * RG:(g + 1) * RG]
            f0 = 0
            while f0 < FF:
                fw = min(BW, FF - f0)
                h1 = dot(xe, w1b[:, f0:f0 + fw])
                h3 = dot(xe, w3b[:, f0:f0 + fw])
                act[g, :, f0:f0 + fw] = (h1 * jax.nn.sigmoid(h1) * h3).astype(BF)
                f0 += fw

        def down(g, d):
            ys[l, g, d] = dot(act[g], w2b[pool_of(d)])

        def relay_add(g):
            for way in range(2):
                relay_send(g, way).wait_recv()
                ysum[l, g, way] = ys[l, g, 1 if way == 0 else 3, way * RH:(way + 1) * RH] + rlr[l, g, way]
                sum_send(g, way).start()

        def finish(g):
            for way in range(2):
                direct_send(g, 1 - way).wait_recv()
                sum_send(g, way).wait_recv()
                rows = slice(way * RH, (way + 1) * RH)
                tot = ys[l, g, 0, rows] + drr[l, g, 1 - way] + srr[l, g, way]
                ybf[l, g * RG + way * RH:g * RG + (way + 1) * RH] = tot.astype(BF)
            for dp_ in (2, 1, 3, 0):
                for r in range((g + 1) * NR // 2 - 1, g * NR // 2 - 1, -1):
                    if dp_ or r:
                        ret_send(dp_, r).start()
            if g == 0:
                yret[l, p, pl.ds(pl.multiple_of(e * RE, RE), RE), :] = ybf[l, 0:RE, :]

        with jax.named_scope("up0"):
            up(0)
        with jax.named_scope("down0"):
            wait(down_copies(l))
            down(0, 2)
            for way in range(2):
                relay_send(0, way).start()
            down(0, 1)
            direct_send(0, 0).start()
            down(0, 3)
            direct_send(0, 1).start()
            down(0, 0)
        with jax.named_scope("up1"):
            up(1)

            @pl.when(more)
            def _():
                start(up_copies(l + 1))

        with jax.named_scope("down1"):
            down(1, 2)
            for way in range(2):
                relay_send(1, way).start()
            relay_add(0)
            down(1, 1)
            direct_send(1, 0).start()
            down(1, 3)
            direct_send(1, 1).start()
            down(1, 0)

            @pl.when(more)
            def _():
                start(down_copies(l + 1))

        with jax.named_scope("relay1"):
            relay_add(1)
        with jax.named_scope("finish0"):
            finish(0)
        with jax.named_scope("finish1"):
            finish(1)
        with jax.named_scope("retwait"):
            for dp_ in range(NP):
                for r in range(NR):
                    if dp_ or r:
                        ret_send(dp_, r).wait_recv()

        with jax.named_scope("gsum"):
            for b in range(NP):
                cols = slice(b * CB, (b + 1) * CB)
                yp = dot(rmat, yret[l, b]) * gcol
                mixed = yp[0:T]
                for k in range(1, K):
                    mixed = mixed + yp[k * T:(k + 1) * T]
                xs[:, cols] = (a_s[:, cols] + mixed).astype(BF).astype(F32)

        for half in range(2):
            for i in range(NP - 1):
                att_send(half, i).wait_send()
                og_send(half, i + 1).wait_send()
        for r in range(1, NR):
            dis_send(r).wait_send()
        for g in range(2):
            for way in range(2):
                relay_send(g, way).wait_send()
                direct_send(g, way).wait_send()
                sum_send(g, way).wait_send()
        for dp_ in range(NP):
            for r in range(NR):
                if dp_ or r:
                    ret_send(dp_, r).wait_send()
        return carry

    lax.fori_loop(0, L, layer, 0)
    out_ref[...] = xs[...].astype(BF)


def solution(mesh):
    tok_spec = P(("dp", "ep"), None)
    cache_spec = P(None, ("dp", "ep"), "pool", None, None)
    up_spec = P(None, "ep", None, "pool")
    down_spec = P(None, "ep", "pool", None)
    in_specs = (tok_spec, cache_spec, cache_spec, P(("dp", "ep")), P(), P(), P(), P(), P(),
                P(None, ("dp", "ep"), None), up_spec, up_spec, down_spec)
    NP, NE = mesh.shape["pool"], mesh.shape["ep"]

    def body(hidden, k_cache, v_cache, cache_len, w_q, w_k, w_v, w_o, w_router, ids, w_one, w_three, w_two):
        L = w_q.shape[0]
        T, D = hidden.shape
        S, G, HD = k_cache.shape[2:]
        NH = w_q.shape[2] // HD
        K = ids.shape[2]
        FF = w_one.shape[3]
        TC = T // NP
        SLOTS, CB, ROWS, SG, UR = T * K, D // NP, TC * NH, S * G, TC // 2 * NH
        assert w_one.shape[1] == 1 and SLOTS == HD and ROWS == HD and w_router.shape[2] == 8 and NP == 4 and G == 2
        dims = (L, T, D, S, G, HD, NH, NP, NE, TC, K, FF)
        kc = k_cache.reshape(L, T, SG, HD)
        vc = v_cache.reshape(L, T, SG, HD)
        wr_t = jnp.swapaxes(w_router, 1, 2)
        ids_t = jnp.swapaxes(ids, 1, 2)
        V = pltpu.VMEM
        dma = pltpu.SemaphoreType.DMA
        anyspec = pl.BlockSpec(memory_space=pl.ANY)
        vspec = pl.BlockSpec(memory_space=pltpu.VMEM)
        scratch = [
            V((T, D), BF), V((T, D), F32), V(ids_t.shape, jnp.int32), V(wr_t.shape, F32),
            V((NH // 2 + G, D, 2 * HD), BF),
            V((2 * NP, TC // 2, SG, HD), BF), V((2 * NP, TC // 2, SG, HD), BF), V((D, D), BF),
            V((D, FF), BF), V((D, FF), BF), V((NP, FF, CB), BF),
            V((T * NH, HD), F32), V((T, 2 * G * HD), F32), V((ROWS, HD), F32), V((ROWS, HD), F32),
            V((ROWS, HD), F32), V((L, 2, NP, UR + 8, HD), F32), V((L, 2, NP - 1, UR + 8, HD), F32),
            V((UR, HD), F32), V((L, T, NH * HD), BF),
            V((T, D), F32), V((L, SLOTS, D), BF), V((L, SLOTS, D), BF), V((2, SLOTS // 2, FF), BF),
            V((L, 2, NP, SLOTS // 2, CB), F32), V((L, 2, 2, SLOTS // 4, CB), F32),
            V((L, 2, 2, SLOTS // 4, CB), F32), V((L, 2, 2, SLOTS // 4, CB), F32), V((L, 2, 2, SLOTS // 4, CB), F32),
            V((L, SLOTS, CB), BF), V((L, NP, SLOTS, CB), BF),
            dma((NH // 2 + G + 6 + NP,)), dma((2, 2 * NP)),
            dma((L, 2, NP - 1)), dma((L, 2, NP - 1)), dma((L, 2, NP - 1)), dma((L, 2, NP - 1)),
            dma((L, NE)), dma((L, NE)),
            dma((L, 2, 2)), dma((L, 2, 2)), dma((L, 2, 2)), dma((L, 2, 2)), dma((L, 2, 2)), dma((L, 2, 2)),
            dma((L, NP, NE)), dma((L, NP, NE)),
        ]
        return pl.pallas_call(
            functools.partial(layers_kernel, dims),
            out_shape=jax.ShapeDtypeStruct((T, D), BF),
            in_specs=[pl.BlockSpec(memory_space=pltpu.SMEM), anyspec, anyspec, anyspec, anyspec, anyspec, anyspec,
                      anyspec, anyspec, anyspec, anyspec, anyspec, anyspec],
            out_specs=vspec,
            scratch_shapes=scratch,
            name="moe_layers",
            compiler_params=pltpu.CompilerParams(collective_id=0, has_side_effects=True,
                                                 vmem_limit_bytes=60 * 1024 * 1024),
        )(cache_len, hidden, ids_t, kc, vc, w_q, w_k, w_v, w_o, wr_t, w_one, w_three, w_two)

    return jax.shard_map(body, mesh=mesh, in_specs=in_specs, out_specs=tok_spec, check_vma=False)
```

time: 363 us -> 86.4 us (0.24)
  blocking collectives: 88.9 us -> 0 us
  local copies, waits for them, and re-layouts: 54.2 us -> 1.57 us
  Pallas kernels: 38.6 us -> 84.7 us
  starting transfers between devices: 46.1 us -> 0 us
  waiting for transfers between devices: 45.9 us -> 0 us
  other arithmetic: 43.3 us -> 0 us
  matrix products: 30.6 us -> 0 us
  between operations: 14.2 us -> 0.01 us
    pallas_call x0 -> x1, Pallas kernels: none -> 84.7 us  [body(): pl.pallas_call(functools.partial(layers_kernel, dims), out_shape=jax.Shap...]
    psum x4 -> x0, blocking collectives: 60.7 us -> none  [the longest x2 36.1 us: expert_math(): return lax.psum(part_out, 'pool').astype(jnp.bfloat16)]
    all_to_all x6 -> x0, starting transfers between devices: 46.1 us -> none  [the longest x2 17.3 us: body(): back_rows = lax.all_to_all(expert_rows, 'ep', 0, 0, tiled=True)]
    another operation x6 -> x0, Pallas kernels: 36.2 us -> none
    dot_general x16 -> x0, matrix products: 30.6 us -> none  [the longest x2 11.7 us: attention_block(): jnp.einsum('tgqd,tsgd->tgqs', query, k_rows, preferred_element_type=jnp.f...]
    slice x5 -> x0, local copies, waits for them, and re-layouts: 28.3 us -> none  [the longest x1 14.1 us: body(): k_cache[layer_idx]]
    pmax x2 -> x0, blocking collectives: 28.2 us -> none  [attention_block(): lax.pmax(jnp.max(score_vals, axis=-1), 'pool')]
    psum x2 -> x0, waiting for transfers between devices: 23.5 us -> none  [attention_block(): lax.psum(jnp.einsum('tgqs,tsgd->tgqd', prob_vals.astype(jnp.bfloat16), v_...]
  transfers between devices with their start and end apart: 8 -> 0, of which waited for: 5 -> 0; matrix products, arithmetic and copies ran while one was open for 12% -> 0% of each run, Pallas kernels for 1% -> 0%
where the time goes in v2:
time: 86.4 us; the launch traced here: 86.3 us
  Pallas kernels  84.7 us (98%)
  local copies, waits for them, and re-layouts  1.57 us (2%)
    pallas_call x1, Pallas kernels, body(): pl.pallas_call(functools.partial(layers_kernel, dims), out_shape=jax.Shap...  84.7 us

profile of v2, /device:TPU:97, one launch (start us, length us, event | category | flops | bytes accessed | tf_op | source)
XLA Modules:
  0.0 86.3 jit_solution(4594225046394973340)
XLA Ops:
  0.0 84.7 %moe_layers.1 = bf16[64,1024]{1,0:T(8,128)(2,1)} custom-call(s32[64]{0:T(128)} %len_ref.1, bf16[64,1024]{1,0:T(8,128)(2,1)} %x_hbm.1, s32[2,2,64]{2,1,0:T(2,128)} %bitcast.7, bf16[2,64,512,128]{3,2,1,0:T(8,128)(2,1)} %bitcast.4, bf16[2,64,512,128]{3,2,1,0:T(8,128)(2,1)} %bitcast.5, bf16[2,1024,1024]{2,1,0:T(8,128)(2,1)} %wq_hbm.1, ...), custom_call_target="tpu_custom_call" | custom-call | tf_op jit(solution)/shard_map/moe_layers/pallas_call | solution.py:515
  84.7 1.6 %copy.15 = bf16[64,1024]{1,0:T(8,128)(2,1)} copy(bf16[64,1024]{1,0:T(8,128)(2,1)} %moe_layers.1) | data formatting | bytes 262144

commit v3 on v2

v3 whole, which is shorter than its diff:
```python
import functools

import jax
import jax.numpy as jnp
from jax import lax
from jax.experimental import pallas as pl
from jax.experimental.pallas import tpu as pltpu
from jax.sharding import PartitionSpec as P

MESH = pl.DeviceIdType.MESH
NORM_EPS = 1e-6
NEG = -1e30
BF = jnp.bfloat16
F32 = jnp.float32
NT = (((1,), (1,)), ((), ()))


def rms_norm(v):
    return v * lax.rsqrt(jnp.mean(v * v, axis=-1, keepdims=True) + NORM_EPS)


def dot(a, b):
    return jnp.dot(a, b, preferred_element_type=F32)


def layers_kernel(dims, len_ref, x_hbm, ids_hbm, k_hbm, v_hbm, wq_hbm, wk_hbm, wv_hbm, wo_hbm, wr_hbm,
                  w1_hbm, w3_hbm, w2_hbm, out_ref,
                  xb, xs, idb, wrb, wqb, wkvb, kvbuf, wob, w1b, w3b, w2b, qrows, kvs, kx, vx, zst, msg, arx, orow, oag,
                  a_s, uperm, xin, act, ys, yrecv, ybf, yret,
                  ld_sem, kv_sem, att_s, att_r, og_s, og_r, dis_s, dis_r, ys_s, ys_r, ret_s, ret_r):
    L, T, D, S, G, HD, NH, NP, NE, TC, K, FF = dims
    QG = NH // G
    SLOTS = T * K
    RE = SLOTS // NE
    CB = D // NP
    SG = S * G
    QW = NH * HD
    KW = G * HD
    TU = TC // 2
    TH = T // 2
    UR = TU * NH
    NU = 2 * NP
    NM = 2 * (NP - 1)
    NX = NE // 2
    RG = SLOTS // 2
    BW = 2 * HD
    scale = HD ** -0.5
    p = lax.axis_index("pool")
    e = lax.axis_index("ep")
    chip = lax.div(e, 2)
    core = lax.rem(e, 2)

    def pool_of(d):
        return lax.rem(p + d, NP)

    rel = [(0, 0), (0, 1), (1, 0), (NX - 1, 0), (1, 1), (NX - 1, 1)]
    rel += [(dx, dc) for dx in range(2, NX - 1) for dc in range(2)]
    NR = len(rel)

    def ep_sender(r):
        return lax.rem(chip + rel[r][0], NX) * 2 + lax.rem(core + rel[r][1], 2)

    def ep_receiver(r):
        return lax.rem(chip + NX - rel[r][0], NX) * 2 + lax.rem(core + rel[r][1], 2)

    def qkv_load(l):
        for b in range(2):
            rows = pl.ds(b * (D // 2), D // 2)
            pltpu.make_async_copy(wq_hbm.at[l, rows], wqb.at[rows], ld_sem.at[0]).start()
        pltpu.make_async_copy(wk_hbm.at[l], wkvb.at[0], ld_sem.at[1]).start()
        pltpu.make_async_copy(wv_hbm.at[l], wkvb.at[1], ld_sem.at[1]).start()

    def drain(ref, sem):
        pltpu.make_async_copy(ref, ref, sem).wait()

    def unit(n):
        z = n // NM
        half = (1 - z) * (n // (NP - 1)) + z * (n - NM)
        away = (1 - z) * (n % (NP - 1) + 1)
        return half, away

    def unit_tok(n):
        half, away = unit(n)
        return half * TH + lax.rem(p + away, NP) * TU

    def kv_load(l, n):
        tok = pl.ds(pl.multiple_of(unit_tok(n), TU), TU)
        pltpu.make_async_copy(k_hbm.at[l, tok], kvbuf.at[n, 0], kv_sem.at[n]).start()
        pltpu.make_async_copy(v_hbm.at[l, tok], kvbuf.at[n, 1], kv_sem.at[n]).start()

    def wo_copy(l):
        return pltpu.make_async_copy(wo_hbm.at[l], wob, ld_sem.at[2])

    def up_load(l):
        pltpu.make_async_copy(w1_hbm.at[l, 0], w1b, ld_sem.at[3]).start()
        pltpu.make_async_copy(w3_hbm.at[l, 0], w3b, ld_sem.at[4]).start()

    def down_load(l):
        for q in range(NP):
            pltpu.make_async_copy(w2_hbm.at[l, 0, :, pl.ds(q * CB, CB)], w2b.at[q], ld_sem.at[5]).start()

    small = [pltpu.make_async_copy(x_hbm, xb, ld_sem.at[6]),
             pltpu.make_async_copy(ids_hbm, idb, ld_sem.at[7]),
             pltpu.make_async_copy(wr_hbm, wrb, ld_sem.at[8])]
    small[0].start()
    qkv_load(0)
    for n in range(2):
        kv_load(0, n)
    small[1].start()
    small[2].start()

    barrier = pltpu.get_barrier_semaphore()
    for dp_ in range(NP):
        for de in range(NE):
            if dp_ or de:
                pl.semaphore_signal(barrier, inc=1,
                                    device_id={"pool": pool_of(dp_), "ep": lax.rem(e + de, NE)},
                                    device_id_type=MESH)

    hrow = lax.broadcasted_iota(jnp.int32, (NH, SG), 0)
    pcol = lax.broadcasted_iota(jnp.int32, (NH, SG), 1)
    posm = jnp.where(lax.rem(pcol, G) == lax.div(hrow, QG), lax.div(pcol, G), jnp.int32(1 << 30))
    lane = lax.broadcasted_iota(jnp.int32, (NH, HD), 1)
    NEX = wrb.shape[1]
    ecol = lax.broadcasted_iota(jnp.int32, (NEX, T), 0)

    small[0].wait()
    xs[...] = xb[...].astype(F32)

    def layer(l, carry):
        more = l + 1 < L
        first = l == 0

        def att_send(n, away):
            return pltpu.make_async_remote_copy(
                src_ref=msg.at[l, n], dst_ref=arx.at[l, n], send_sem=att_s, recv_sem=att_r.at[n // (NP - 1)],
                device_id={"pool": pool_of(away), "ep": e}, device_id_type=MESH)

        def own_tok(half):
            return pl.ds(pl.multiple_of(half * TH + p * TU, TU), TU)

        def og_send(half, d):
            return pltpu.make_async_remote_copy(
                src_ref=oag.at[l, own_tok(half)], dst_ref=oag.at[l, own_tok(half)], send_sem=og_s, recv_sem=og_r,
                device_id={"pool": pool_of(d), "ep": e}, device_id_type=MESH)

        def dis_send(r):
            dst = ep_receiver(r)
            return pltpu.make_async_remote_copy(
                src_ref=uperm.at[l, pl.ds(pl.multiple_of(dst * RE, RE), RE)], dst_ref=xin.at[l, pl.ds(r * RE, RE)],
                send_sem=dis_s, recv_sem=dis_r.at[r // (NR // 2)],
                device_id={"pool": p, "ep": dst}, device_id_type=MESH)

        def ys_send(g, d):
            return pltpu.make_async_remote_copy(
                src_ref=ys.at[l, g, d - 1], dst_ref=yrecv.at[l, g, d - 1], send_sem=ys_s.at[g],
                recv_sem=ys_r.at[g], device_id={"pool": pool_of(d), "ep": e}, device_id_type=MESH)

        def ret_send(dp_, r):
            dst = ep_sender(r)
            return pltpu.make_async_remote_copy(
                src_ref=ybf.at[l, pl.ds(r * RE, RE)],
                dst_ref=yret.at[l, pl.ds(pl.multiple_of(p * SLOTS + e * RE, RE), RE)], send_sem=ret_s, recv_sem=ret_r,
                device_id={"pool": pool_of(dp_), "ep": dst}, device_id_type=MESH)

        with jax.named_scope("qkv"):
            hn = rms_norm(xs[...]).astype(BF)
            drain(wqb, ld_sem.at[0])
            for b in range(QW // BW):
                r = dot(hn, wqb[:, b * BW:(b + 1) * BW]).astype(BF).astype(F32)
                for j in range(2):
                    qrows[pl.ds(2 * b + j, T, stride=NH), :] = r[:, j * HD:(j + 1) * HD]
            drain(wkvb, ld_sem.at[1])
            for b in range(2):
                kvs[:, b * KW:(b + 1) * KW] = dot(hn, wkvb[b]).astype(BF).astype(F32)

            @pl.when(first)
            def _():
                for n in range(2, 4):
                    kv_load(l, n)

            for half in range(2):
                for h in range(NH):
                    g = h // QG
                    kx[pl.ds(half * UR + h, TU, stride=NH), :] = kvs[own_tok(half), g * HD:(g + 1) * HD]
                    vx[pl.ds(half * UR + h, TU, stride=NH), :] = kvs[own_tok(half), KW + g * HD:KW + (g + 1) * HD]

        def merge(qrow, krow, stats, parts):
            s_new = jnp.sum(qrow * kx[krow, :], axis=1, keepdims=True) * scale
            ms = [c[:, 0:1] for c in stats]
            top = s_new
            for m in ms:
                top = jnp.maximum(top, m)
            p_new = jnp.exp(s_new - top)
            den = p_new
            num = p_new * vx[krow, :]
            for i in range(NP):
                w = jnp.exp(ms[i] - top)
                den = den + w * stats[i][:, 1:2]
                num = num + w * parts[i]
            return num / den

        def combine(half):
            m0 = half * (NP - 1)
            drain(arx.at[l, pl.ds(m0, NP - 1)], att_r.at[half])
            for i in range(NP - 1):
                zst[8 * i:8 * i + 8, :] = arx[l, m0 + i, UR:UR + 8, :]
            zst[8 * (NP - 1):8 * NP, :] = msg[l, NM + half, UR:UR + 8, :]
            zc = zst[...].T
            odd = [(m0 + i) % 2 for i in range(NP - 1)] + [(NM + half) % 2]
            stats = [zc[odd[i] * UR:(odd[i] + 1) * UR, 8 * i:8 * i + 8] for i in range(NP)]
            parts = [arx[l, m0 + i, 0:UR, :] for i in range(NP - 1)] + [msg[l, NM + half, 0:UR, :]]
            q0 = pl.multiple_of((half * TH + p * TU) * NH, UR)
            orow[...] = merge(qrows[pl.ds(q0, UR), :], pl.ds(half * UR, UR), stats, parts)
            for h in range(NH):
                oag[l, own_tok(half), h * HD:(h + 1) * HD] = orow[pl.ds(h, TU, stride=NH), :].astype(BF)
            for d in (2, 1, 3):
                og_send(half, d).start()

        def chunk(it, c2):
            for un in range(2):
                n = 2 * it + un
                drain(kvbuf.at[n], kv_sem.at[n])

            @pl.when(jnp.logical_and(first, it < 2))
            def _():
                for un in range(2):
                    kv_load(l, 2 * it + 4 + un)

            @pl.when(jnp.logical_and(first, it == 2))
            def _():
                wo_copy(l).start()
                up_load(l)
                down_load(l)

            for un in range(2):
                n = 2 * it + un
                t0 = unit_tok(n)
                sc = []
                for j in range(TU):
                    t = t0 + j
                    qt = qrows[pl.ds(pl.multiple_of(t * NH, NH), NH), :].astype(BF)
                    s = lax.dot_general(qt, kvbuf[n, 0, j], NT, preferred_element_type=F32) * scale
                    sc.append(jnp.where(posm < len_ref[t] - p * S, s, NEG))
                mx = [jnp.max(s, axis=1, keepdims=True) for s in sc]
                pr = [jnp.exp(s - m) for s, m in zip(sc, mx)]
                ls = [jnp.sum(q, axis=1, keepdims=True) for q in pr]
                for j in range(TU):
                    msg[l, n, j * NH:(j + 1) * NH, :] = dot(pr[j].astype(BF), kvbuf[n, 1, j])
                    zst[un * UR + j * NH:un * UR + (j + 1) * NH, :] = jnp.where(lane == 0, mx[j], ls[j])
            zt = zst[...].T[0:8, :]
            for un in range(2):
                msg[l, 2 * it + un, UR:UR + 8, :] = zt

            @pl.when(jnp.logical_and(first, it == 0))
            def _():
                pl.semaphore_wait(barrier, NP * NE - 1)

            @pl.when(it < NP - 1)
            def _():
                for un in range(2):
                    n = 2 * it + un
                    att_send(n, unit(n)[1]).start()

            return c2

        with jax.named_scope("attn"):
            lax.fori_loop(0, NP, chunk, 0)

        @pl.when(more)
        def _():
            qkv_load(l + 1)
            for n in range(NU):
                kv_load(l + 1, n)

        @pl.when(first)
        def _():
            small[1].wait()
            small[2].wait()

        with jax.named_scope("tables"):
            slot_col = lax.broadcasted_iota(jnp.int32, (SLOTS, SLOTS), 0)
            pair_row = lax.broadcasted_iota(jnp.int32, (SLOTS, SLOTS), 1)
            upper = (slot_col < pair_row).astype(F32).astype(BF)
            want_rank = lax.rem(slot_col, RE).astype(F32)
            idrow = jnp.concatenate([idb[l, k:k + 1, :] for k in range(K)], axis=1)
            same = (jnp.broadcast_to(idrow, (SLOTS, SLOTS)) == lax.div(slot_col, RE))
            rank = dot(same.astype(F32).astype(BF), upper)
            pick = jnp.where(jnp.logical_and(same, rank == want_rank), 1.0, 0.0).astype(F32)
            rmat = pick.T.astype(BF)
            dmat = pick[:, 0:T]
            for k in range(1, K):
                dmat = dmat + pick[:, k * T:(k + 1) * T]
            dmat = dmat.astype(BF)
            wr = wrb[l]
            hi = wr.astype(BF).astype(F32)
            mid = (wr - hi).astype(BF).astype(F32)
            lo = wr - hi - mid
            wr3 = jnp.concatenate([hi, mid, lo, jnp.zeros_like(lo)], axis=0).astype(BF)

        with jax.named_scope("comb0"):
            combine(0)
        with jax.named_scope("comb1"):
            combine(1)
        with jax.named_scope("agwait"):
            wo_copy(l).wait()
            drain(oag.at[l, pl.ds(0, NM * TU)], og_r)

        with jax.named_scope("oproj"):
            for b in range(NP):
                cols = slice(b * CB, (b + 1) * CB)
                a_s[:, cols] = (xs[:, cols] + dot(oag[l], wob[:, cols])).astype(BF).astype(F32)

            @pl.when(more)
            def _():
                wo_copy(l + 1).start()

            u = rms_norm(a_s[...]).astype(BF)
            for b in range(NP):
                cols = slice(b * CB, (b + 1) * CB)
                uperm[l, :, cols] = dot(dmat, u[:, cols]).astype(BF)
            for r in range(1, NR):
                dis_send(r).start()
            xin[l, 0:RE, :] = uperm[l, pl.ds(pl.multiple_of(e * RE, RE), RE), :]

        with jax.named_scope("gates"):
            lg3 = lax.dot_general(wr3, u, NT, preferred_element_type=F32)
            lg = lg3[0:NEX] + lg3[NEX:2 * NEX] + lg3[2 * NEX:3 * NEX]
            picked = [jnp.sum(jnp.where(ecol == idb[l, k:k + 1, :], lg, 0.0), axis=0, keepdims=True)
                      for k in range(K)]
            gtop = picked[0]
            for k in range(1, K):
                gtop = jnp.maximum(gtop, picked[k])
            ex = [jnp.exp(v - gtop) for v in picked]
            tot = ex[0]
            for k in range(1, K):
                tot = tot + ex[k]
            grow = jnp.concatenate([v / tot for v in ex], axis=1)
            gcol = jnp.broadcast_to(grow, (SLOTS, SLOTS)).T[:, 0:1]
            drain(w1b, ld_sem.at[3])
            drain(w3b, ld_sem.at[4])

        def up(g):
            r0 = 1 if g == 0 else NR // 2
            drain(xin.at[l, pl.ds(r0 * RE, (NR // 2 - (g == 0)) * RE)], dis_r.at[g])
            xe = xin[l, g * RG:(g + 1) * RG]
            f0 = 0
            while f0 < FF:
                fw = min(BW, FF - f0)
                h1 = dot(xe, w1b[:, f0:f0 + fw])
                h3 = dot(xe, w3b[:, f0:f0 + fw])
                act[g, :, f0:f0 + fw] = (h1 * jax.nn.sigmoid(h1) * h3).astype(BF)
                f0 += fw

        def down(g, d):
            ys[l, g, (d + NP - 1) % NP] = dot(act[g], w2b[pool_of(d)])

        def finish(g):
            drain(yrecv.at[l, g], ys_r.at[g])
            tot = ys[l, g, NP - 1]
            for d in range(1, NP):
                tot = tot + yrecv[l, g, d - 1]
            ybf[l, g * RG:(g + 1) * RG] = tot.astype(BF)
            for dp_ in (2, 1, 3, 0):
                for r in range((g + 1) * NR // 2 - 1, g * NR // 2 - 1, -1):
                    if dp_ or r:
                        ret_send(dp_, r).start()
            if g == 0:
                yret[l, pl.ds(pl.multiple_of(p * SLOTS + e * RE, RE), RE), :] = ybf[l, 0:RE, :]

        def down_all(g):
            for d in (2, 1, 3, 0):
                down(g, d)
                if d:
                    ys_send(g, d).start()

        with jax.named_scope("up0"):
            up(0)
        with jax.named_scope("down0"):
            drain(w2b, ld_sem.at[5])
            down_all(0)
        with jax.named_scope("up1"):
            up(1)

            @pl.when(more)
            def _():
                up_load(l + 1)

        with jax.named_scope("down1"):
            down_all(1)

            @pl.when(more)
            def _():
                down_load(l + 1)

        with jax.named_scope("finish0"):
            finish(0)
        with jax.named_scope("finish1"):
            finish(1)
        all_ret = yret.at[l, pl.ds(0, (NP * NE - 1) * RE)]
        with jax.named_scope("retwait"):
            drain(all_ret, ret_r)

        with jax.named_scope("gsum"):
            for b in range(NP):
                cols = slice(b * CB, (b + 1) * CB)
                yp = dot(rmat, yret[l, b * SLOTS:(b + 1) * SLOTS]) * gcol
                mixed = yp[0:T]
                for k in range(1, K):
                    mixed = mixed + yp[k * T:(k + 1) * T]
                xs[:, cols] = (a_s[:, cols] + mixed).astype(BF).astype(F32)

        drain(msg.at[l, pl.ds(0, NM)], att_s)
        drain(oag.at[l, pl.ds(0, NM * TU)], og_s)
        drain(uperm.at[l, pl.ds(0, (NR - 1) * RE)], dis_s)
        for g in range(2):
            drain(ys.at[l, g, pl.ds(0, NP - 1)], ys_s.at[g])
        drain(all_ret, ret_s)
        return carry

    lax.fori_loop(0, L, layer, 0)
    out_ref[...] = xs[...].astype(BF)


def solution(mesh):
    tok_spec = P(("dp", "ep"), None)
    cache_spec = P(None, ("dp", "ep"), "pool", None, None)
    up_spec = P(None, "ep", None, "pool")
    down_spec = P(None, "ep", "pool", None)
    in_specs = (tok_spec, cache_spec, cache_spec, P(("dp", "ep")), P(), P(), P(), P(), P(),
                P(None, ("dp", "ep"), None), up_spec, up_spec, down_spec)
    NP, NE = mesh.shape["pool"], mesh.shape["ep"]

    def body(hidden, k_cache, v_cache, cache_len, w_q, w_k, w_v, w_o, w_router, ids, w_one, w_three, w_two):
        L = w_q.shape[0]
        T, D = hidden.shape
        S, G, HD = k_cache.shape[2:]
        NH = w_q.shape[2] // HD
        K = ids.shape[2]
        FF = w_one.shape[3]
        TC = T // NP
        SLOTS, CB, ROWS, SG, UR = T * K, D // NP, TC * NH, S * G, TC // 2 * NH
        assert w_one.shape[1] == 1 and SLOTS == HD and ROWS == HD and w_router.shape[2] == 8 and NP == 4 and G == 2
        dims = (L, T, D, S, G, HD, NH, NP, NE, TC, K, FF)
        kc = k_cache.reshape(L, T, SG, HD)
        vc = v_cache.reshape(L, T, SG, HD)
        wr_t = jnp.swapaxes(w_router, 1, 2)
        ids_t = jnp.swapaxes(ids, 1, 2)
        V = pltpu.VMEM
        dma = pltpu.SemaphoreType.DMA
        anyspec = pl.BlockSpec(memory_space=pl.ANY)
        vspec = pl.BlockSpec(memory_space=pltpu.VMEM)
        scratch = [
            V((T, D), BF), V((T, D), F32), V(ids_t.shape, jnp.int32), V(wr_t.shape, F32),
            V((D, NH * HD), BF), V((2, D, G * HD), BF), V((2 * NP, 2, TC // 2, SG, HD), BF), V((D, D), BF),
            V((D, FF), BF), V((D, FF), BF), V((NP, FF, CB), BF),
            V((T * NH, HD), F32), V((T, 2 * G * HD), F32), V((ROWS, HD), F32), V((ROWS, HD), F32),
            V((ROWS, HD), F32), V((L, 2 * NP, UR + 8, HD), F32), V((L, 2 * NP - 2, UR + 8, HD), F32),
            V((UR, HD), F32), V((L, T, NH * HD), BF),
            V((T, D), F32), V((L, SLOTS, D), BF), V((L, SLOTS, D), BF), V((2, SLOTS // 2, FF), BF),
            V((L, 2, NP, SLOTS // 2, CB), F32), V((L, 2, NP - 1, SLOTS // 2, CB), F32),
            V((L, SLOTS, CB), BF), V((L, NP * SLOTS, CB), BF),
            dma((9,)), dma((2 * NP,)), dma, dma((2,)), dma, dma, dma, dma((2,)), dma((2,)), dma((2,)), dma, dma,
        ]
        return pl.pallas_call(
            functools.partial(layers_kernel, dims),
            out_shape=jax.ShapeDtypeStruct((T, D), BF),
            in_specs=[pl.BlockSpec(memory_space=pltpu.SMEM), anyspec, anyspec, anyspec, anyspec, anyspec, anyspec,
                      anyspec, anyspec, anyspec, anyspec, anyspec, anyspec],
            out_specs=vspec,
            scratch_shapes=scratch,
            name="moe_layers",
            compiler_params=pltpu.CompilerParams(collective_id=0, has_side_effects=True,
                                                 vmem_limit_bytes=60 * 1024 * 1024),
        )(cache_len, hidden, ids_t, kc, vc, w_q, w_k, w_v, w_o, wr_t, w_one, w_three, w_two)

    return jax.shard_map(body, mesh=mesh, in_specs=in_specs, out_specs=tok_spec, check_vma=False)
```

time: 86.4 us -> 71.9 us (0.83)
  Pallas kernels: 84.7 us -> 70.2 us
    pallas_call x1, Pallas kernels: 84.7 us -> 70.2 us  [body(): pl.pallas_call(functools.partial(layers_kernel, dims), out_shape=jax.Shap...]
where the time goes in v3:
time: 71.9 us; the launch traced here: 71.8 us
  Pallas kernels  70.2 us (98%)
  local copies, waits for them, and re-layouts  1.57 us (2%)
    pallas_call x1, Pallas kernels, body(): pl.pallas_call(functools.partial(layers_kernel, dims), out_shape=jax.Shap...  70.2 us
    unnamed x1, local copies, waits for them, and re-layouts  1.57 us

profile of v3, /device:TPU:97, one launch (start us, length us, event | category | flops | bytes accessed | tf_op | source)
XLA Modules:
  0.0 71.8 jit_solution(15003280451702742877)
XLA Ops:
  0.0 70.2 %moe_layers.1 = bf16[64,1024]{1,0:T(8,128)(2,1)} custom-call(s32[64]{0:T(128)} %len_ref.1, bf16[64,1024]{1,0:T(8,128)(2,1)} %x_hbm.1, s32[2,2,64]{2,1,0:T(2,128)} %bitcast.7, bf16[2,64,512,128]{3,2,1,0:T(8,128)(2,1)} %bitcast.4, bf16[2,64,512,128]{3,2,1,0:T(8,128)(2,1)} %bitcast.5, bf16[2,1024,1024]{2,1,0:T(8,128)(2,1)} %wq_hbm.1, ...), custom_call_target="tpu_custom_call" | custom-call | tf_op jit(solution)/shard_map/moe_layers/pallas_call | solution.py:465
  70.2 1.6 %copy.15 = bf16[64,1024]{1,0:T(8,128)(2,1)} copy(bf16[64,1024]{1,0:T(8,128)(2,1)} %moe_layers.1) | data formatting | bytes 262144

commit v4 on v3

--- a/solution.py
+++ b/solution.py
@@ -42,7 +42,6 @@
     NU = 2 * NP
     NM = 2 * (NP - 1)
     NX = NE // 2
-    RG = SLOTS // 2
     BW = 2 * HD
     scale = HD ** -0.5
     p = lax.axis_index("pool")
@@ -53,9 +52,12 @@
     def pool_of(d):
         return lax.rem(p + d, NP)
 
-    rel = [(0, 0), (0, 1), (1, 0), (NX - 1, 0), (1, 1), (NX - 1, 1)]
-    rel += [(dx, dc) for dx in range(2, NX - 1) for dc in range(2)]
+    rel = [(0, 0), (0, 1)] + [(dx, dc) for dx in range(2, NX - 1) for dc in range(2)]
+    rel += [(1, 0), (NX - 1, 0), (1, 1), (NX - 1, 1)]
     NR = len(rel)
+    groups = [(0, 2), (2, 4), (4, NR)]
+    NG = len(groups)
+    group_of = [next(g for g in range(NG) if r < groups[g][1]) for r in range(NR)]
 
     def ep_sender(r):
         return lax.rem(chip + rel[r][0], NX) * 2 + lax.rem(core + rel[r][1], 2)
@@ -73,18 +75,19 @@
     def drain(ref, sem):
         pltpu.make_async_copy(ref, ref, sem).wait()
 
-    def unit(n):
-        z = n // NM
-        half = (1 - z) * (n // (NP - 1)) + z * (n - NM)
-        away = (1 - z) * (n % (NP - 1) + 1)
+    def unit(it, un):
+        z = (it + 1) // 2 % 2
+        half = z * (it - 1) + (1 - z) * un
+        away = z * (1 + 2 * un) + (1 - z) * (2 - 2 * (it // 3))
         return half, away
 
-    def unit_tok(n):
-        half, away = unit(n)
+    def unit_tok(it, un):
+        half, away = unit(it, un)
         return half * TH + lax.rem(p + away, NP) * TU
 
-    def kv_load(l, n):
-        tok = pl.ds(pl.multiple_of(unit_tok(n), TU), TU)
+    def kv_load(l, it, un):
+        n = 2 * it + un
+        tok = pl.ds(pl.multiple_of(unit_tok(it, un), TU), TU)
         pltpu.make_async_copy(k_hbm.at[l, tok], kvbuf.at[n, 0], kv_sem.at[n]).start()
         pltpu.make_async_copy(v_hbm.at[l, tok], kvbuf.at[n, 1], kv_sem.at[n]).start()
 
@@ -104,8 +107,8 @@
              pltpu.make_async_copy(wr_hbm, wrb, ld_sem.at[8])]
     small[0].start()
     qkv_load(0)
-    for n in range(2):
-        kv_load(0, n)
+    for un in range(2):
+        kv_load(0, 0, un)
     small[1].start()
     small[2].start()
 
@@ -121,6 +124,7 @@
     pcol = lax.broadcasted_iota(jnp.int32, (NH, SG), 1)
     posm = jnp.where(lax.rem(pcol, G) == lax.div(hrow, QG), lax.div(pcol, G), jnp.int32(1 << 30))
     lane = lax.broadcasted_iota(jnp.int32, (NH, HD), 1)
+    hsub = lax.broadcasted_iota(jnp.int32, (NH, HD), 0)
     NEX = wrb.shape[1]
     ecol = lax.broadcasted_iota(jnp.int32, (NEX, T), 0)
 
@@ -131,9 +135,11 @@
         more = l + 1 < L
         first = l == 0
 
-        def att_send(n, away):
+        def att_send(it, un):
+            half, away = unit(it, un)
             return pltpu.make_async_remote_copy(
-                src_ref=msg.at[l, n], dst_ref=arx.at[l, n], send_sem=att_s, recv_sem=att_r.at[n // (NP - 1)],
+                src_ref=msg.at[l, 2 * it + un], dst_ref=arx.at[l, half * (NP - 1) + away - 1], send_sem=att_s,
+                recv_sem=att_r.at[half],
                 device_id={"pool": pool_of(away), "ep": e}, device_id_type=MESH)
 
         def own_tok(half):
@@ -148,12 +154,15 @@
             dst = ep_receiver(r)
             return pltpu.make_async_remote_copy(
                 src_ref=uperm.at[l, pl.ds(pl.multiple_of(dst * RE, RE), RE)], dst_ref=xin.at[l, pl.ds(r * RE, RE)],
-                send_sem=dis_s, recv_sem=dis_r.at[r // (NR // 2)],
+                send_sem=dis_s, recv_sem=dis_r.at[group_of[r]],
                 device_id={"pool": p, "ep": dst}, device_id_type=MESH)
+
+        def grows(g):
+            return pl.ds(groups[g][0] * RE, (groups[g][1] - groups[g][0]) * RE)
 
         def ys_send(g, d):
             return pltpu.make_async_remote_copy(
-                src_ref=ys.at[l, g, d - 1], dst_ref=yrecv.at[l, g, d - 1], send_sem=ys_s.at[g],
+                src_ref=ys.at[l, d - 1, grows(g)], dst_ref=yrecv.at[l, d - 1, grows(g)], send_sem=ys_s.at[g],
                 recv_sem=ys_r.at[g], device_id={"pool": pool_of(d), "ep": e}, device_id_type=MESH)
 
         def ret_send(dp_, r):
@@ -176,8 +185,8 @@
 
             @pl.when(first)
             def _():
-                for n in range(2, 4):
-                    kv_load(l, n)
+                for un in range(2):
+                    kv_load(l, 1, un)
 
             for half in range(2):
                 for h in range(NH):
@@ -207,7 +216,7 @@
                 zst[8 * i:8 * i + 8, :] = arx[l, m0 + i, UR:UR + 8, :]
             zst[8 * (NP - 1):8 * NP, :] = msg[l, NM + half, UR:UR + 8, :]
             zc = zst[...].T
-            odd = [(m0 + i) % 2 for i in range(NP - 1)] + [(NM + half) % 2]
+            odd = [0, half, 1, half]
             stats = [zc[odd[i] * UR:(odd[i] + 1) * UR, 8 * i:8 * i + 8] for i in range(NP)]
             parts = [arx[l, m0 + i, 0:UR, :] for i in range(NP - 1)] + [msg[l, NM + half, 0:UR, :]]
             q0 = pl.multiple_of((half * TH + p * TU) * NH, UR)
@@ -225,7 +234,7 @@
             @pl.when(jnp.logical_and(first, it < 2))
             def _():
                 for un in range(2):
-                    kv_load(l, 2 * it + 4 + un)
+                    kv_load(l, it + 2, un)
 
             @pl.when(jnp.logical_and(first, it == 2))
             def _():
@@ -233,9 +242,11 @@
                 up_load(l)
                 down_load(l)
 
+            mrow = jnp.zeros((NH, HD), F32)
+            lrow = jnp.zeros((NH, HD), F32)
             for un in range(2):
                 n = 2 * it + un
-                t0 = unit_tok(n)
+                t0 = unit_tok(it, un)
                 sc = []
                 for j in range(TU):
                     t = t0 + j
@@ -247,10 +258,12 @@
                 ls = [jnp.sum(q, axis=1, keepdims=True) for q in pr]
                 for j in range(TU):
                     msg[l, n, j * NH:(j + 1) * NH, :] = dot(pr[j].astype(BF), kvbuf[n, 1, j])
-                    zst[un * UR + j * NH:un * UR + (j + 1) * NH, :] = jnp.where(lane == 0, mx[j], ls[j])
-            zt = zst[...].T[0:8, :]
+                    here = lane == hsub + (un * UR + j * NH)
+                    mrow = jnp.where(here, mx[j], mrow)
+                    lrow = jnp.where(here, ls[j], lrow)
+            stat = jnp.where(hsub == 0, jnp.sum(mrow, axis=0, keepdims=True), jnp.sum(lrow, axis=0, keepdims=True))
             for un in range(2):
-                msg[l, 2 * it + un, UR:UR + 8, :] = zt
+                msg[l, 2 * it + un, UR:UR + NH, :] = stat
 
             @pl.when(jnp.logical_and(first, it == 0))
             def _():
@@ -259,8 +272,7 @@
             @pl.when(it < NP - 1)
             def _():
                 for un in range(2):
-                    n = 2 * it + un
-                    att_send(n, unit(n)[1]).start()
+                    att_send(it, un).start()
 
             return c2
 
@@ -271,7 +283,7 @@
         def _():
             qkv_load(l + 1)
             for n in range(NU):
-                kv_load(l + 1, n)
+                kv_load(l + 1, n // 2, n % 2)
 
         @pl.when(first)
         def _():
@@ -341,62 +353,53 @@
             drain(w3b, ld_sem.at[4])
 
         def up(g):
-            r0 = 1 if g == 0 else NR // 2
-            drain(xin.at[l, pl.ds(r0 * RE, (NR // 2 - (g == 0)) * RE)], dis_r.at[g])
-            xe = xin[l, g * RG:(g + 1) * RG]
+            r0 = max(1, groups[g][0])
+            drain(xin.at[l, pl.ds(r0 * RE, (groups[g][1] - r0) * RE)], dis_r.at[g])
+            xe = xin[l, grows(g)]
             f0 = 0
             while f0 < FF:
                 fw = min(BW, FF - f0)
                 h1 = dot(xe, w1b[:, f0:f0 + fw])
                 h3 = dot(xe, w3b[:, f0:f0 + fw])
-                act[g, :, f0:f0 + fw] = (h1 * jax.nn.sigmoid(h1) * h3).astype(BF)
+                act[grows(g), f0:f0 + fw] = (h1 * jax.nn.sigmoid(h1) * h3).astype(BF)
                 f0 += fw
 
-        def down(g, d):
-            ys[l, g, (d + NP - 1) % NP] = dot(act[g], w2b[pool_of(d)])
+        def down(g):
+            for d in (2, 1, 3, 0):
+                ys[l, (d + NP - 1) % NP, grows(g)] = dot(act[grows(g)], w2b[pool_of(d)])
+            for d in (2, 1, 3):
+                ys_send(g, d).start()
 
         def finish(g):
-            drain(yrecv.at[l, g], ys_r.at[g])
-            tot = ys[l, g, NP - 1]
+            drain(yrecv.at[l, :, grows(g)], ys_r.at[g])
+            tot = ys[l, NP - 1, grows(g)]
             for d in range(1, NP):
-                tot = tot + yrecv[l, g, d - 1]
-            ybf[l, g * RG:(g + 1) * RG] = tot.astype(BF)
+                tot = tot + yrecv[l, d - 1, grows(g)]
+            ybf[l, grows(g)] = tot.astype(BF)
             for dp_ in (2, 1, 3, 0):
-                for r in range((g + 1) * NR // 2 - 1, g * NR // 2 - 1, -1):
+                for r in range(groups[g][1] - 1, groups[g][0] - 1, -1):
                     if dp_ or r:
                         ret_send(dp_, r).start()
             if g == 0:
                 yret[l, pl.ds(pl.multiple_of(p * SLOTS + e * RE, RE), RE), :] = ybf[l, 0:RE, :]
 
-        def down_all(g):
-            for d in (2, 1, 3, 0):
-                down(g, d)
-                if d:
-                    ys_send(g, d).start()
-
-        with jax.named_scope("up0"):
-            up(0)
-        with jax.named_scope("down0"):
-            drain(w2b, ld_sem.at[5])
-            down_all(0)
-        with jax.named_scope("up1"):
-            up(1)
-
-            @pl.when(more)
-            def _():
-                up_load(l + 1)
-
-        with jax.named_scope("down1"):
-            down_all(1)
-
-            @pl.when(more)
-            def _():
-                down_load(l + 1)
-
-        with jax.named_scope("finish0"):
-            finish(0)
-        with jax.named_scope("finish1"):
-            finish(1)
+        for g in range(NG):
+            with jax.named_scope(f"up{g}"):
+                up(g)
+            if g == 0:
+                drain(w2b, ld_sem.at[5])
+            with jax.named_scope(f"down{g}"):
+                down(g)
+
+        @pl.when(more)
+        def _():
+            up_load(l + 1)
+            down_load(l + 1)
+
+        for g in range(NG):
+            with jax.named_scope(f"finish{g}"):
+                finish(g)
+
         all_ret = yret.at[l, pl.ds(0, (NP * NE - 1) * RE)]
         with jax.named_scope("retwait"):
             drain(all_ret, ret_r)
@@ -413,8 +416,8 @@
         drain(msg.at[l, pl.ds(0, NM)], att_s)
         drain(oag.at[l, pl.ds(0, NM * TU)], og_s)
         drain(uperm.at[l, pl.ds(0, (NR - 1) * RE)], dis_s)
-        for g in range(2):
-            drain(ys.at[l, g, pl.ds(0, NP - 1)], ys_s.at[g])
+        for g in range(NG):
+            drain(ys.at[l, pl.ds(0, NP - 1), grows(g)], ys_s.at[g])
         drain(all_ret, ret_s)
         return carry
 
@@ -446,6 +449,7 @@
         vc = v_cache.reshape(L, T, SG, HD)
         wr_t = jnp.swapaxes(w_router, 1, 2)
         ids_t = jnp.swapaxes(ids, 1, 2)
+        NG = 3
         V = pltpu.VMEM
         dma = pltpu.SemaphoreType.DMA
         anyspec = pl.BlockSpec(memory_space=pl.ANY)
@@ -457,14 +461,14 @@
             V((T * NH, HD), F32), V((T, 2 * G * HD), F32), V((ROWS, HD), F32), V((ROWS, HD), F32),
             V((ROWS, HD), F32), V((L, 2 * NP, UR + 8, HD), F32), V((L, 2 * NP - 2, UR + 8, HD), F32),
             V((UR, HD), F32), V((L, T, NH * HD), BF),
-            V((T, D), F32), V((L, SLOTS, D), BF), V((L, SLOTS, D), BF), V((2, SLOTS // 2, FF), BF),
-            V((L, 2, NP, SLOTS // 2, CB), F32), V((L, 2, NP - 1, SLOTS // 2, CB), F32),
+            V((T, D), F32), V((L, SLOTS, D), BF), V((L, SLOTS, D), BF), V((SLOTS, FF), BF),
+            V((L, NP, SLOTS, CB), F32), V((L, NP - 1, SLOTS, CB), F32),
             V((L, SLOTS, CB), BF), V((L, NP * SLOTS, CB), BF),
-            dma((9,)), dma((2 * NP,)), dma, dma((2,)), dma, dma, dma, dma((2,)), dma((2,)), dma((2,)), dma, dma,
+            dma((9,)), dma((2 * NP,)), dma, dma((2,)), dma, dma, dma, dma((NG,)), dma((NG,)), dma((NG,)), dma, dma,
         ]
         return pl.pallas_call(
             functools.partial(layers_kernel, dims),
-            out_shape=jax.ShapeDtypeStruct((T, D), BF),
+            out_shape=pltpu.VMEM((T, D), BF),
             in_specs=[pl.BlockSpec(memory_space=pltpu.SMEM), anyspec, anyspec, anyspec, anyspec, anyspec, anyspec,
                       anyspec, anyspec, anyspec, anyspec, anyspec, anyspec],
             out_specs=vspec,

time: 71.9 us -> 68.2 us (0.949)
  Pallas kernels: 70.2 us -> 67.4 us
  local copies, waits for them, and re-layouts: 1.57 us -> 0.66 us
    pallas_call x1, Pallas kernels: 70.2 us -> 67.4 us  [body(): pl.pallas_call(functools.partial(layers_kernel, dims), out_shape=pltpu.VM...]
    unnamed x1, local copies, waits for them, and re-layouts: 1.57 us -> 0.66 us
where the time goes in v4:
time: 68.2 us; the launch traced here: 68.1 us
  Pallas kernels  67.4 us (99%)
    pallas_call x1, Pallas kernels, body(): pl.pallas_call(functools.partial(layers_kernel, dims), out_shape=pltpu.VM...  67.4 us

profile of v4, /device:TPU:97, one launch (start us, length us, event | category | flops | bytes accessed | tf_op | source)
XLA Modules:
  0.0 68.1 jit_solution(17785906367104063658)
XLA Ops:
  0.0 67.4 %moe_layers.1 = bf16[64,1024]{1,0:T(8,128)(2,1)S(1)} custom-call(s32[64]{0:T(128)} %len_ref.1, bf16[64,1024]{1,0:T(8,128)(2,1)} %x_hbm.1, s32[2,2,64]{2,1,0:T(2,128)} %bitcast.7, bf16[2,64,512,128]{3,2,1,0:T(8,128)(2,1)} %bitcast.4, bf16[2,64,512,128]{3,2,1,0:T(8,128)(2,1)} %bitcast.5, bf16[2,1024,1024]{2,1,0:T(8,128)(2,1)} %wq_hbm.1, ...), custom_call_target="tpu_custom_call" | custom-call | tf_op jit(solution)/shard_map/moe_layers/pallas_call | solution.py:469
  67.4 0.7 copy.15

commit v5 on v4

--- a/solution.py
+++ b/solution.py
@@ -25,7 +25,7 @@
 
 def layers_kernel(dims, len_ref, x_hbm, ids_hbm, k_hbm, v_hbm, wq_hbm, wk_hbm, wv_hbm, wo_hbm, wr_hbm,
                   w1_hbm, w3_hbm, w2_hbm, out_ref,
-                  xb, xs, idb, wrb, wqb, wkvb, kvbuf, wob, w1b, w3b, w2b, qrows, kvs, kx, vx, zst, msg, arx, orow, oag,
+                  xb, xs, hb, idb, wrb, wqb, wkvb, kvbuf, wob, w1b, w3b, w2b, qrows, kvs, kx, vx, zst, msg, arx, orow, oag,
                   a_s, uperm, xin, act, ys, yrecv, ybf, yret,
                   ld_sem, kv_sem, att_s, att_r, og_s, og_r, dis_s, dis_r, ys_s, ys_r, ret_s, ret_r):
     L, T, D, S, G, HD, NH, NP, NE, TC, K, FF = dims
@@ -55,9 +55,9 @@
     rel = [(0, 0), (0, 1)] + [(dx, dc) for dx in range(2, NX - 1) for dc in range(2)]
     rel += [(1, 0), (NX - 1, 0), (1, 1), (NX - 1, 1)]
     NR = len(rel)
-    groups = [(0, 2), (2, 4), (4, NR)]
+    groups = [(0, 2), (2, 4), (4, 6), (6, NR)]
     NG = len(groups)
-    group_of = [next(g for g in range(NG) if r < groups[g][1]) for r in range(NR)]
+    group_of = [next(g for g in range(NG) if groups[g][0] <= r < groups[g][1]) for r in range(NR)]
 
     def ep_sender(r):
         return lax.rem(chip + rel[r][0], NX) * 2 + lax.rem(core + rel[r][1], 2)
@@ -65,10 +65,12 @@
     def ep_receiver(r):
         return lax.rem(chip + NX - rel[r][0], NX) * 2 + lax.rem(core + rel[r][1], 2)
 
-    def qkv_load(l):
+    def wq_load(l):
         for b in range(2):
             rows = pl.ds(b * (D // 2), D // 2)
             pltpu.make_async_copy(wq_hbm.at[l, rows], wqb.at[rows], ld_sem.at[0]).start()
+
+    def wkv_load(l):
         pltpu.make_async_copy(wk_hbm.at[l], wkvb.at[0], ld_sem.at[1]).start()
         pltpu.make_async_copy(wv_hbm.at[l], wkvb.at[1], ld_sem.at[1]).start()
 
@@ -106,7 +108,7 @@
              pltpu.make_async_copy(ids_hbm, idb, ld_sem.at[7]),
              pltpu.make_async_copy(wr_hbm, wrb, ld_sem.at[8])]
     small[0].start()
-    qkv_load(0)
+    wq_load(0)
     for un in range(2):
         kv_load(0, 0, un)
     small[1].start()
@@ -179,20 +181,13 @@
                 r = dot(hn, wqb[:, b * BW:(b + 1) * BW]).astype(BF).astype(F32)
                 for j in range(2):
                     qrows[pl.ds(2 * b + j, T, stride=NH), :] = r[:, j * HD:(j + 1) * HD]
-            drain(wkvb, ld_sem.at[1])
-            for b in range(2):
-                kvs[:, b * KW:(b + 1) * KW] = dot(hn, wkvb[b]).astype(BF).astype(F32)
+            hb[...] = hn
 
             @pl.when(first)
             def _():
                 for un in range(2):
                     kv_load(l, 1, un)
-
-            for half in range(2):
-                for h in range(NH):
-                    g = h // QG
-                    kx[pl.ds(half * UR + h, TU, stride=NH), :] = kvs[own_tok(half), g * HD:(g + 1) * HD]
-                    vx[pl.ds(half * UR + h, TU, stride=NH), :] = kvs[own_tok(half), KW + g * HD:KW + (g + 1) * HD]
+                wkv_load(l)
 
         def merge(qrow, krow, stats, parts):
             s_new = jnp.sum(qrow * kx[krow, :], axis=1, keepdims=True) * scale
@@ -279,9 +274,21 @@
         with jax.named_scope("attn"):
             lax.fori_loop(0, NP, chunk, 0)
 
+        with jax.named_scope("kvproj"):
+            drain(wkvb, ld_sem.at[1])
+            for b in range(2):
+                kvs[:, b * KW:(b + 1) * KW] = dot(hb[...], wkvb[b]).astype(BF).astype(F32)
+
+            for half in range(2):
+                for h in range(NH):
+                    g = h // QG
+                    kx[pl.ds(half * UR + h, TU, stride=NH), :] = kvs[own_tok(half), g * HD:(g + 1) * HD]
+                    vx[pl.ds(half * UR + h, TU, stride=NH), :] = kvs[own_tok(half), KW + g * HD:KW + (g + 1) * HD]
+
         @pl.when(more)
         def _():
-            qkv_load(l + 1)
+            wq_load(l + 1)
+            wkv_load(l + 1)
             for n in range(NU):
                 kv_load(l + 1, n // 2, n % 2)
 
@@ -449,13 +456,13 @@
         vc = v_cache.reshape(L, T, SG, HD)
         wr_t = jnp.swapaxes(w_router, 1, 2)
         ids_t = jnp.swapaxes(ids, 1, 2)
-        NG = 3
+        NG = 4
         V = pltpu.VMEM
         dma = pltpu.SemaphoreType.DMA
         anyspec = pl.BlockSpec(memory_space=pl.ANY)
         vspec = pl.BlockSpec(memory_space=pltpu.VMEM)
         scratch = [
-            V((T, D), BF), V((T, D), F32), V(ids_t.shape, jnp.int32), V(wr_t.shape, F32),
+            V((T, D), BF), V((T, D), F32), V((T, D), BF), V(ids_t.shape, jnp.int32), V(wr_t.shape, F32),
             V((D, NH * HD), BF), V((2, D, G * HD), BF), V((2 * NP, 2, TC // 2, SG, HD), BF), V((D, D), BF),
             V((D, FF), BF), V((D, FF), BF), V((NP, FF, CB), BF),
             V((T * NH, HD), F32), V((T, 2 * G * HD), F32), V((ROWS, HD), F32), V((ROWS, HD), F32),

time: 68.2 us -> 67.4 us (0.988)
  Pallas kernels: 67.4 us -> 66.7 us
    pallas_call x1, Pallas kernels: 67.4 us -> 66.7 us  [body(): pl.pallas_call(functools.partial(layers_kernel, dims), out_shape=pltpu.VM...]
where the time goes in v5:
time: 67.4 us; the launch traced here: 67.3 us
  Pallas kernels  66.7 us (99%)
    pallas_call x1, Pallas kernels, body(): pl.pallas_call(functools.partial(layers_kernel, dims), out_shape=pltpu.VM...  66.7 us

profile of v5, /device:TPU:97, one launch (start us, length us, event | category | flops | bytes accessed | tf_op | source)
XLA Modules:
  0.0 67.3 jit_solution(6681982255603321705)
XLA Ops:
  0.0 66.7 %moe_layers.1 = bf16[64,1024]{1,0:T(8,128)(2,1)S(1)} custom-call(s32[64]{0:T(128)} %len_ref.1, bf16[64,1024]{1,0:T(8,128)(2,1)} %x_hbm.1, s32[2,2,64]{2,1,0:T(2,128)} %bitcast.7, bf16[2,64,512,128]{3,2,1,0:T(8,128)(2,1)} %bitcast.4, bf16[2,64,512,128]{3,2,1,0:T(8,128)(2,1)} %bitcast.5, bf16[2,1024,1024]{2,1,0:T(8,128)(2,1)} %wq_hbm.1, ...), custom_call_target="tpu_custom_call" | custom-call | tf_op jit(solution)/shard_map/moe_layers/pallas_call | solution.py:476
  66.7 0.7 copy.15

commit v6 on v5

--- a/solution.py
+++ b/solution.py
@@ -23,9 +23,9 @@
     return jnp.dot(a, b, preferred_element_type=F32)
 
 
-def layers_kernel(dims, len_ref, x_hbm, ids_hbm, k_hbm, v_hbm, wq_hbm, wk_hbm, wv_hbm, wo_hbm, wr_hbm,
+def layers_kernel(dims, len_hbm, x_hbm, ids_hbm, k_hbm, v_hbm, wq_hbm, wk_hbm, wv_hbm, wo_hbm, wr_hbm,
                   w1_hbm, w3_hbm, w2_hbm, out_ref,
-                  xb, xs, hb, idb, wrb, wqb, wkvb, kvbuf, wob, w1b, w3b, w2b, qrows, kvs, kx, vx, zst, msg, arx, orow, oag,
+                  len_ref, xb, xs, hb, idb, wrb, wqb, wkvb, kvbuf, wob, w1b, w3b, w2b, qrows, kvs, kx, vx, zst, msg, arx, orow, oag,
                   a_s, uperm, xin, act, ys, yrecv, ybf, yret,
                   ld_sem, kv_sem, att_s, att_r, og_s, og_r, dis_s, dis_r, ys_s, ys_r, ret_s, ret_r):
     L, T, D, S, G, HD, NH, NP, NE, TC, K, FF = dims
@@ -106,8 +106,10 @@
 
     small = [pltpu.make_async_copy(x_hbm, xb, ld_sem.at[6]),
              pltpu.make_async_copy(ids_hbm, idb, ld_sem.at[7]),
-             pltpu.make_async_copy(wr_hbm, wrb, ld_sem.at[8])]
+             pltpu.make_async_copy(wr_hbm, wrb, ld_sem.at[8]),
+             pltpu.make_async_copy(len_hbm, len_ref, ld_sem.at[9])]
     small[0].start()
+    small[3].start()
     wq_load(0)
     for un in range(2):
         kv_load(0, 0, un)
@@ -177,6 +179,11 @@
         with jax.named_scope("qkv"):
             hn = rms_norm(xs[...]).astype(BF)
             drain(wqb, ld_sem.at[0])
+
+            @pl.when(first)
+            def _():
+                small[3].wait()
+
             for b in range(QW // BW):
                 r = dot(hn, wqb[:, b * BW:(b + 1) * BW]).astype(BF).astype(F32)
                 for j in range(2):
@@ -187,7 +194,8 @@
             def _():
                 for un in range(2):
                     kv_load(l, 1, un)
-                wkv_load(l)
+                for un in range(2):
+                    kv_load(l, 2, un)
 
         def merge(qrow, krow, stats, parts):
             s_new = jnp.sum(qrow * kx[krow, :], axis=1, keepdims=True) * scale
@@ -226,13 +234,14 @@
                 n = 2 * it + un
                 drain(kvbuf.at[n], kv_sem.at[n])
 
-            @pl.when(jnp.logical_and(first, it < 2))
+            @pl.when(jnp.logical_and(first, it == 0))
             def _():
                 for un in range(2):
-                    kv_load(l, it + 2, un)
+                    kv_load(l, 3, un)
 
             @pl.when(jnp.logical_and(first, it == 2))
             def _():
+                wkv_load(l)
                 wo_copy(l).start()
                 up_load(l)
                 down_load(l)
@@ -462,6 +471,7 @@
         anyspec = pl.BlockSpec(memory_space=pl.ANY)
         vspec = pl.BlockSpec(memory_space=pltpu.VMEM)
         scratch = [
+            pltpu.SMEM((T,), jnp.int32),
             V((T, D), BF), V((T, D), F32), V((T, D), BF), V(ids_t.shape, jnp.int32), V(wr_t.shape, F32),
             V((D, NH * HD), BF), V((2, D, G * HD), BF), V((2 * NP, 2, TC // 2, SG, HD), BF), V((D, D), BF),
             V((D, FF), BF), V((D, FF), BF), V((NP, FF, CB), BF),
@@ -471,12 +481,12 @@
             V((T, D), F32), V((L, SLOTS, D), BF), V((L, SLOTS, D), BF), V((SLOTS, FF), BF),
             V((L, NP, SLOTS, CB), F32), V((L, NP - 1, SLOTS, CB), F32),
             V((L, SLOTS, CB), BF), V((L, NP * SLOTS, CB), BF),
-            dma((9,)), dma((2 * NP,)), dma, dma((2,)), dma, dma, dma, dma((NG,)), dma((NG,)), dma((NG,)), dma, dma,
+            dma((10,)), dma((2 * NP,)), dma, dma((2,)), dma, dma, dma, dma((NG,)), dma((NG,)), dma((NG,)), dma, dma,
         ]
         return pl.pallas_call(
             functools.partial(layers_kernel, dims),
             out_shape=pltpu.VMEM((T, D), BF),
-            in_specs=[pl.BlockSpec(memory_space=pltpu.SMEM), anyspec, anyspec, anyspec, anyspec, anyspec, anyspec,
+            in_specs=[anyspec, anyspec, anyspec, anyspec, anyspec, anyspec, anyspec,
                       anyspec, anyspec, anyspec, anyspec, anyspec, anyspec],
             out_specs=vspec,
             scratch_shapes=scratch,

time: 67.4 us -> 66.5 us (0.987)
  Pallas kernels: 66.7 us -> 65.8 us
    pallas_call x1, Pallas kernels: 66.7 us -> 65.8 us  [body(): pl.pallas_call(functools.partial(layers_kernel, dims), out_shape=pltpu.VM...]
where the time goes in v6:
time: 66.5 us; the launch traced here: 66.4 us
  Pallas kernels  65.8 us (99%)
    pallas_call x1, Pallas kernels, body(): pl.pallas_call(functools.partial(layers_kernel, dims), out_shape=pltpu.VM...  65.8 us

profile of v6, /device:TPU:97, one launch (start us, length us, event | category | flops | bytes accessed | tf_op | source)
XLA Modules:
  0.0 66.4 jit_solution(12806974171387086795)
XLA Ops:
  0.0 65.8 %moe_layers.1 = bf16[64,1024]{1,0:T(8,128)(2,1)S(1)} custom-call(s32[64]{0:T(128)} %len_hbm.1, bf16[64,1024]{1,0:T(8,128)(2,1)} %x_hbm.1, s32[2,2,64]{2,1,0:T(2,128)} %bitcast.7, bf16[2,64,512,128]{3,2,1,0:T(8,128)(2,1)} %bitcast.4, bf16[2,64,512,128]{3,2,1,0:T(8,128)(2,1)} %bitcast.5, bf16[2,1024,1024]{2,1,0:T(8,128)(2,1)} %wq_hbm.1, ...), custom_call_target="tpu_custom_call" | custom-call | tf_op jit(solution)/shard_map/moe_layers/pallas_call | solution.py:486
  65.8 0.7 copy.15

commit v7 on v6

--- a/solution.py
+++ b/solution.py
@@ -130,8 +130,12 @@
     lane = lax.broadcasted_iota(jnp.int32, (NH, HD), 1)
     hsub = lax.broadcasted_iota(jnp.int32, (NH, HD), 0)
     NEX = wrb.shape[1]
+    hlane = lax.rem(lane, UR)
+    row_lane = lax.rem(lax.broadcasted_iota(jnp.int32, (UR, HD), 1), UR)
+    row_id = lax.broadcasted_iota(jnp.int32, (UR, HD), 0)
     ecol = lax.broadcasted_iota(jnp.int32, (NEX, T), 0)
 
+    zst[...] = jnp.zeros_like(zst)
     small[0].wait()
     xs[...] = xb[...].astype(F32)
 
@@ -197,39 +201,38 @@
                 for un in range(2):
                     kv_load(l, 2, un)
 
-        def merge(qrow, krow, stats, parts):
-            s_new = jnp.sum(qrow * kx[krow, :], axis=1, keepdims=True) * scale
-            ms = [c[:, 0:1] for c in stats]
+        def new_scores(half):
+            q0 = pl.multiple_of((half * TH + p * TU) * NH, UR)
+            krow = pl.ds(half * UR, UR)
+            s_new = jnp.sum(qrows[pl.ds(q0, UR), :] * kx[krow, :], axis=1, keepdims=True) * scale
+            return jnp.sum(jnp.where(row_lane == row_id, s_new, 0.0), axis=0, keepdims=True)
+
+        def combine(half, s_new):
+            m0 = half * (NP - 1)
+            drain(arx.at[l, pl.ds(m0, NP - 1)], att_r.at[half])
+            parts = [arx.at[l, m0 + i] for i in range(NP - 1)] + [msg.at[l, 2 * (NP - 1) + half]]
+            ms = [ref[UR:UR + 1, :] for ref in parts]
             top = s_new
             for m in ms:
                 top = jnp.maximum(top, m)
-            p_new = jnp.exp(s_new - top)
-            den = p_new
-            num = p_new * vx[krow, :]
+            w = [jnp.exp(m - top) for m in ms] + [jnp.exp(s_new - top)]
+            den = w[NP]
             for i in range(NP):
-                w = jnp.exp(ms[i] - top)
-                den = den + w * stats[i][:, 1:2]
-                num = num + w * parts[i]
-            return num / den
-
-        def combine(half):
-            m0 = half * (NP - 1)
-            drain(arx.at[l, pl.ds(m0, NP - 1)], att_r.at[half])
-            for i in range(NP - 1):
-                zst[8 * i:8 * i + 8, :] = arx[l, m0 + i, UR:UR + 8, :]
-            zst[8 * (NP - 1):8 * NP, :] = msg[l, NM + half, UR:UR + 8, :]
+                den = den + w[i] * parts[i][UR + 1:UR + 2, :]
+            inv = 1.0 / den
+            for i in range(NP + 1):
+                zst[i:i + 1, :] = w[i] * inv
             zc = zst[...].T
-            odd = [0, half, 1, half]
-            stats = [zc[odd[i] * UR:(odd[i] + 1) * UR, 8 * i:8 * i + 8] for i in range(NP)]
-            parts = [arx[l, m0 + i, 0:UR, :] for i in range(NP - 1)] + [msg[l, NM + half, 0:UR, :]]
-            q0 = pl.multiple_of((half * TH + p * TU) * NH, UR)
-            orow[...] = merge(qrows[pl.ds(q0, UR), :], pl.ds(half * UR, UR), stats, parts)
+            out = zc[0:UR, NP:NP + 1] * vx[pl.ds(half * UR, UR), :]
+            for i in range(NP):
+                out = out + zc[0:UR, i:i + 1] * parts[i][0:UR, :]
+            orow[...] = out
             for h in range(NH):
                 oag[l, own_tok(half), h * HD:(h + 1) * HD] = orow[pl.ds(h, TU, stride=NH), :].astype(BF)
             for d in (2, 1, 3):
                 og_send(half, d).start()
 
-        def chunk(it, c2):
+        def attend(it, send):
             for un in range(2):
                 n = 2 * it + un
                 drain(kvbuf.at[n], kv_sem.at[n])
@@ -246,8 +249,6 @@
                 up_load(l)
                 down_load(l)
 
-            mrow = jnp.zeros((NH, HD), F32)
-            lrow = jnp.zeros((NH, HD), F32)
             for un in range(2):
                 n = 2 * it + un
                 t0 = unit_tok(it, un)
@@ -260,28 +261,30 @@
                 mx = [jnp.max(s, axis=1, keepdims=True) for s in sc]
                 pr = [jnp.exp(s - m) for s, m in zip(sc, mx)]
                 ls = [jnp.sum(q, axis=1, keepdims=True) for q in pr]
+                mrow = jnp.zeros((NH, HD), F32)
+                lrow = jnp.zeros((NH, HD), F32)
                 for j in range(TU):
                     msg[l, n, j * NH:(j + 1) * NH, :] = dot(pr[j].astype(BF), kvbuf[n, 1, j])
-                    here = lane == hsub + (un * UR + j * NH)
+                    here = hlane == hsub + j * NH
                     mrow = jnp.where(here, mx[j], mrow)
                     lrow = jnp.where(here, ls[j], lrow)
-            stat = jnp.where(hsub == 0, jnp.sum(mrow, axis=0, keepdims=True), jnp.sum(lrow, axis=0, keepdims=True))
-            for un in range(2):
-                msg[l, 2 * it + un, UR:UR + NH, :] = stat
-
-            @pl.when(jnp.logical_and(first, it == 0))
-            def _():
-                pl.semaphore_wait(barrier, NP * NE - 1)
-
-            @pl.when(it < NP - 1)
-            def _():
-                for un in range(2):
+                msg[l, n, UR:UR + 1, :] = jnp.sum(mrow, axis=0, keepdims=True)
+                msg[l, n, UR + 1:UR + 2, :] = jnp.sum(lrow, axis=0, keepdims=True)
+                if send and un == 0:
+                    @pl.when(jnp.logical_and(first, it == 0))
+                    def _():
+                        pl.semaphore_wait(barrier, NP * NE - 1)
+
+                if send:
                     att_send(it, un).start()
 
+        def chunk(it, c2):
+            attend(it, True)
             return c2
 
         with jax.named_scope("attn"):
-            lax.fori_loop(0, NP, chunk, 0)
+            lax.fori_loop(0, NP - 1, chunk, 0)
+            attend(NP - 1, False)
 
         with jax.named_scope("kvproj"):
             drain(wkvb, ld_sem.at[1])
@@ -300,6 +303,8 @@
             wkv_load(l + 1)
             for n in range(NU):
                 kv_load(l + 1, n // 2, n % 2)
+
+        new_row = [new_scores(half) for half in range(2)]
 
         @pl.when(first)
         def _():
@@ -327,9 +332,9 @@
             wr3 = jnp.concatenate([hi, mid, lo, jnp.zeros_like(lo)], axis=0).astype(BF)
 
         with jax.named_scope("comb0"):
-            combine(0)
+            combine(0, new_row[0])
         with jax.named_scope("comb1"):
-            combine(1)
+            combine(1, new_row[1])
         with jax.named_scope("agwait"):
             wo_copy(l).wait()
             drain(oag.at[l, pl.ds(0, NM * TU)], og_r)
@@ -476,7 +481,7 @@
             V((D, NH * HD), BF), V((2, D, G * HD), BF), V((2 * NP, 2, TC // 2, SG, HD), BF), V((D, D), BF),
             V((D, FF), BF), V((D, FF), BF), V((NP, FF, CB), BF),
             V((T * NH, HD), F32), V((T, 2 * G * HD), F32), V((ROWS, HD), F32), V((ROWS, HD), F32),
-            V((ROWS, HD), F32), V((L, 2 * NP, UR + 8, HD), F32), V((L, 2 * NP - 2, UR + 8, HD), F32),
+            V((ROWS, HD), F32), V((L, 2 * NP, UR + 2, HD), F32), V((L, 2 * NP - 2, UR + 2, HD), F32),
             V((UR, HD), F32), V((L, T, NH * HD), BF),
             V((T, D), F32), V((L, SLOTS, D), BF), V((L, SLOTS, D), BF), V((SLOTS, FF), BF),
             V((L, NP, SLOTS, CB), F32), V((L, NP - 1, SLOTS, CB), F32),

time: 66.5 us -> 65.9 us (level)
  no operation moved by 1% of the time
where the time goes in v7:
time: 65.9 us; the launch traced here: 65.8 us
  Pallas kernels  65.2 us (99%)
  local copies, waits for them, and re-layouts  0.66 us (1%)
    pallas_call x1, Pallas kernels, body(): pl.pallas_call(functools.partial(layers_kernel, dims), out_shape=pltpu.VM...  65.2 us

profile of v7, /device:TPU:97, one launch (start us, length us, event | category | flops | bytes accessed | tf_op | source)
XLA Modules:
  0.0 65.8 jit_solution(418726257370894023)
XLA Ops:
  0.0 65.2 %moe_layers.1 = bf16[64,1024]{1,0:T(8,128)(2,1)S(1)} custom-call(s32[64]{0:T(128)} %len_hbm.1, bf16[64,1024]{1,0:T(8,128)(2,1)} %x_hbm.1, s32[2,2,64]{2,1,0:T(2,128)} %bitcast.7, bf16[2,64,512,128]{3,2,1,0:T(8,128)(2,1)} %bitcast.4, bf16[2,64,512,128]{3,2,1,0:T(8,128)(2,1)} %bitcast.5, bf16[2,1024,1024]{2,1,0:T(8,128)(2,1)} %wq_hbm.1, ...), custom_call_target="tpu_custom_call" | custom-call | tf_op jit(solution)/shard_map/moe_layers/pallas_call | solution.py:491
  65.2 0.7 copy.15

commit v8 on v7

--- a/solution.py
+++ b/solution.py
@@ -52,12 +52,12 @@
     def pool_of(d):
         return lax.rem(p + d, NP)
 
-    rel = [(0, 0), (0, 1)] + [(dx, dc) for dx in range(2, NX - 1) for dc in range(2)]
-    rel += [(1, 0), (NX - 1, 0), (1, 1), (NX - 1, 1)]
+    rel = [(0, 0), (0, 1), (1, 0), (NX - 1, 0)] + [(dx, dc) for dx in range(2, NX - 1) for dc in range(2)] + [(1, 1), (NX - 1, 1)]
     NR = len(rel)
+    ups = [(0, 2), (2, 4), (4, NR)]
     groups = [(0, 2), (2, 4), (4, 6), (6, NR)]
     NG = len(groups)
-    group_of = [next(g for g in range(NG) if groups[g][0] <= r < groups[g][1]) for r in range(NR)]
+    group_of = [next(g for g in range(len(ups)) if ups[g][0] <= r < ups[g][1]) for r in range(NR)]
 
     def ep_sender(r):
         return lax.rem(chip + rel[r][0], NX) * 2 + lax.rem(core + rel[r][1], 2)
@@ -374,15 +374,16 @@
             drain(w3b, ld_sem.at[4])
 
         def up(g):
-            r0 = max(1, groups[g][0])
-            drain(xin.at[l, pl.ds(r0 * RE, (groups[g][1] - r0) * RE)], dis_r.at[g])
-            xe = xin[l, grows(g)]
+            r0, r1 = max(1, ups[g][0]), ups[g][1]
+            drain(xin.at[l, pl.ds(r0 * RE, (r1 - r0) * RE)], dis_r.at[g])
+            rows = pl.ds(ups[g][0] * RE, (r1 - ups[g][0]) * RE)
+            xe = xin[l, rows]
             f0 = 0
             while f0 < FF:
                 fw = min(BW, FF - f0)
                 h1 = dot(xe, w1b[:, f0:f0 + fw])
                 h3 = dot(xe, w3b[:, f0:f0 + fw])
-                act[grows(g), f0:f0 + fw] = (h1 * jax.nn.sigmoid(h1) * h3).astype(BF)
+                act[rows, f0:f0 + fw] = (h1 * jax.nn.sigmoid(h1) * h3).astype(BF)
                 f0 += fw
 
         def down(g):
@@ -405,8 +406,9 @@
                 yret[l, pl.ds(pl.multiple_of(p * SLOTS + e * RE, RE), RE), :] = ybf[l, 0:RE, :]
 
         for g in range(NG):
-            with jax.named_scope(f"up{g}"):
-                up(g)
+            if g < len(ups):
+                with jax.named_scope(f"up{g}"):
+                    up(g)
             if g == 0:
                 drain(w2b, ld_sem.at[5])
             with jax.named_scope(f"down{g}"):

time: 65.9 us -> 65.3 us (level)
  no operation moved by 1% of the time
where the time goes in v8:
time: 65.3 us
  Pallas kernels  64.6 us (99%)
  local copies, waits for them, and re-layouts  0.66 us (1%)
    pallas_call x1, Pallas kernels, body(): pl.pallas_call(functools.partial(layers_kernel, dims), out_shape=pltpu.VM...  64.6 us

profile of v8, /device:TPU:97, one launch (start us, length us, event | category | flops | bytes accessed | tf_op | source)
XLA Modules:
  0.0 65.3 jit_solution(362320380913973882)
XLA Ops:
  0.0 64.6 %moe_layers.1 = bf16[64,1024]{1,0:T(8,128)(2,1)S(1)} custom-call(s32[64]{0:T(128)} %len_hbm.1, bf16[64,1024]{1,0:T(8,128)(2,1)} %x_hbm.1, s32[2,2,64]{2,1,0:T(2,128)} %bitcast.7, bf16[2,64,512,128]{3,2,1,0:T(8,128)(2,1)} %bitcast.4, bf16[2,64,512,128]{3,2,1,0:T(8,128)(2,1)} %bitcast.5, bf16[2,1024,1024]{2,1,0:T(8,128)(2,1)} %wq_hbm.1, ...), custom_call_target="tpu_custom_call" | custom-call | tf_op jit(solution)/shard_map/moe_layers/pallas_call | solution.py:493
  64.6 0.7 %copy.15 = bf16[64,1024]{1,0:T(8,128)(2,1)} copy(bf16[64,1024]{1,0:T(8,128)(2,1)S(1)} %moe_layers.1) | data formatting | bytes 262144

commit v9 on v8

--- a/solution.py
+++ b/solution.py
@@ -297,13 +297,6 @@
                     kx[pl.ds(half * UR + h, TU, stride=NH), :] = kvs[own_tok(half), g * HD:(g + 1) * HD]
                     vx[pl.ds(half * UR + h, TU, stride=NH), :] = kvs[own_tok(half), KW + g * HD:KW + (g + 1) * HD]
 
-        @pl.when(more)
-        def _():
-            wq_load(l + 1)
-            wkv_load(l + 1)
-            for n in range(NU):
-                kv_load(l + 1, n // 2, n % 2)
-
         new_row = [new_scores(half) for half in range(2)]
 
         @pl.when(first)
@@ -372,6 +365,13 @@
             gcol = jnp.broadcast_to(grow, (SLOTS, SLOTS)).T[:, 0:1]
             drain(w1b, ld_sem.at[3])
             drain(w3b, ld_sem.at[4])
+
+        @pl.when(more)
+        def _():
+            wq_load(l + 1)
+            wkv_load(l + 1)
+            for n in range(NU):
+                kv_load(l + 1, n // 2, n % 2)
 
         def up(g):
             r0, r1 = max(1, ups[g][0]), ups[g][1]

time: 65.3 us -> 65 us (level)
  no operation moved by 1% of the time
where the time goes in v9:
time: 65 us
  Pallas kernels  64.3 us (99%)
  local copies, waits for them, and re-layouts  0.66 us (1%)
    pallas_call x1, Pallas kernels, body(): pl.pallas_call(functools.partial(layers_kernel, dims), out_shape=pltpu.VM...  64.3 us

profile of v9, /device:TPU:97, one launch (start us, length us, event | category | flops | bytes accessed | tf_op | source)
XLA Modules:
  0.0 65.0 jit_solution(11653187295751935270)
XLA Ops:
  0.0 64.3 %moe_layers.1 = bf16[64,1024]{1,0:T(8,128)(2,1)S(1)} custom-call(s32[64]{0:T(128)} %len_hbm.1, bf16[64,1024]{1,0:T(8,128)(2,1)} %x_hbm.1, s32[2,2,64]{2,1,0:T(2,128)} %bitcast.7, bf16[2,64,512,128]{3,2,1,0:T(8,128)(2,1)} %bitcast.4, bf16[2,64,512,128]{3,2,1,0:T(8,128)(2,1)} %bitcast.5, bf16[2,1024,1024]{2,1,0:T(8,128)(2,1)} %wq_hbm.1, ...), custom_call_target="tpu_custom_call" | custom-call | tf_op jit(solution)/shard_map/moe_layers/pallas_call | solution.py:493
  64.3 0.7 %copy.15 = bf16[64,1024]{1,0:T(8,128)(2,1)} copy(bf16[64,1024]{1,0:T(8,128)(2,1)S(1)} %moe_layers.1) | data formatting | bytes 262144
